TPU v7x, 8 devices: a whole 2x2x1 slice. The times are simulated.
8 devices in a mesh: batch: 1 (over z), row: 2 (over y), col: 4 (over x, core).
Axes of the slice: x: 2, y: 2, z: 1, core: 2. Of those that a mesh axis runs over, the one named last changes fastest.
Arguments:
- left_op: bfloat16 [6144, 6144], P(('batch', 'row'), 'col')
- left_start: float32 [6144, 128], P(('batch', 'row', 'col'))
- right_op: bfloat16 [16384, 16384], P(('batch', 'row'), 'col')
- right_start: float32 [16384, 128], P(('batch', 'row', 'col'))
Outputs:
- output 1: float32 [6144, 128], P(('batch', 'row', 'col'))
- output 2: float32 [128, 128], P('batch')
- output 3: float32 [16384, 128], P(('batch', 'row', 'col'))
- output 4: float32 [128, 128], P('batch')
All inputs are finite; a program needn't handle non-finite values.
Results may differ from a plain program's by a relative error of at most 0.001.
Values are sent between devices in bfloat16 or wider.
A program may use at most 1 GiB of HBM per device.

v0:
```python
import jax
import jax.numpy as jnp
from jax import lax
from jax.sharding import PartitionSpec as P

SWEEPS = 4
ROW_CONTRACT = (((0,), (0,)), ((), ()))


def gram_total(lhs_mat, rhs_mat, precision, grid_axes):
    local_gram = lax.dot_general(lhs_mat, rhs_mat, ROW_CONTRACT, precision=precision, preferred_element_type=jnp.float32)
    return lax.psum(local_gram, grid_axes)


def cholqr_step(y_mat, gram_mat):
    chol_low = jnp.linalg.cholesky(gram_mat)
    return lax.linalg.triangular_solve(chol_low, y_mat, left_side=False, lower=True, transpose_a=True)


def orthonormalize(y_sub, total_rows, grid_axes):
    y_half = y_sub.astype(jnp.bfloat16)
    gram_one = gram_total(y_half, y_half, None, grid_axes) / total_rows
    y_one = cholqr_step(y_sub, gram_one)
    gram_two = gram_total(y_one, y_one, lax.Precision.HIGHEST, grid_axes) / total_rows
    return cholqr_step(y_one, gram_two)


def solution(mesh):
    row_size = mesh.shape["row"]
    col_size = mesh.shape["col"]
    grid_axes = ("row", "col")
    perm_pairs = [(src_index, (src_index % row_size) * col_size + src_index // row_size) for src_index in range(row_size * col_size)]

    def apply_op(op_blk, x_sub):
        x_moved = lax.ppermute(x_sub.astype(jnp.bfloat16), grid_axes, perm_pairs)
        x_col = lax.all_gather(x_moved, "row", axis=0, tiled=True)
        partial_prod = jnp.dot(op_blk, x_col, preferred_element_type=jnp.float32)
        return lax.psum_scatter(partial_prod, "col", scatter_dimension=0, tiled=True)

    def iterate_local(op_blk, start_sub):
        total_rows = op_blk.shape[0] * row_size
        x_sub = start_sub
        for sweep_index in range(SWEEPS):
            x_sub = orthonormalize(apply_op(op_blk, x_sub), total_rows, grid_axes)
        z_sub = apply_op(op_blk, x_sub)
        rayleigh = gram_total(x_sub, z_sub, lax.Precision.HIGHEST, grid_axes) / total_rows
        return x_sub, rayleigh

    def local_program(left_op, left_start, right_op, right_start):
        left_basis, left_rayleigh = iterate_local(left_op, left_start)
        right_basis, right_rayleigh = iterate_local(right_op, right_start)
        return left_basis, left_rayleigh, right_basis, right_rayleigh

    op_spec = P(("batch", "row"), "col")
    vec_spec = P(("batch", "row", "col"), None)
    small_spec = P("batch", None)
    return jax.shard_map(local_program, mesh=mesh, in_specs=(op_spec, vec_spec, op_spec, vec_spec), out_specs=(vec_spec, small_spec, vec_spec, small_spec), check_vma=False)
```

profile of v0, /device:TPU:0, one launch (start us, length us, event | category | flops | bytes accessed | tf_op | source)
XLA Modules:
  0.0 1374.7 jit_solution(1529433831632971435)
XLA Ops:
  12.6 39.2 %all_gather.30 = bf16[1536,128]{1,0:T(8,128)(2,1)S(1)} all-gather(bf16[768,128]{1,0:T(8,128)(2,1)S(1)} %collective-permute-done), channel_id=1, replica_groups=mesh['batch'=1,'row'=2,'col'=4] {'row'}, dimensions={0}, use_global_device_ids=true | all-gather | bytes 589824 | tf_op jit(solution)/shard_map/all_gather | solution.py:36
  51.9 7.5 fusion.86
  59.4 29.3 %fusion.92 = f32[8192,128]{1,0:T(8,128)} fusion(bf16[8192,4096]{1,0:T(8,128)(2,1)} %param.11, bf16[4096,128]{1,0:T(8,128)(2,1)} %all-gather.6.cloned.1.call-done), kind=kOutput, calls=%fused_computation.193 | convolution fusion | flops 8589934592 | bytes 72351744 | tf_op jit(solution)/shard_map/dot_general | solution.py:37
  90.9 37.2 %reduce-scatter.21.cloned.1.call-done = f32[2048,128]{1,0:T(8,128)} async-done(((f32[8192,128]{1,0:T(8,128)}), f32[2048,128]{1,0:T(8,128)}) %reduce-scatter.21.cloned.1.call-update) | async-done | bytes 1048592 | tf_op jit(solution)/shard_map/reduce_scatter | solution.py:38
  128.2 2.5 fusion.12
  130.9 42.2 %all-reduce.35.cloned.1.call-done = (f32[128,128]{0,1:T(8,128)}, f32[128,128]{0,1:T(8,128)}) async-done(((f32[128,128]{0,1:T(8,128)}, f32[128,128]{0,1:T(8,128)}), (f32[128,128]{0,1:T(8,128)}, f32[128,128]{0,1:T(8,128)})) %all-reduce.35.cloned.1.call-update) | async-done | bytes 131088 | tf_op jit(solution)/shard_map/psum | solution.py:12
  176.0 11.7 cholesky.254
  189.0 9.8 custom-call.22
  201.5 11.7 cholesky.342
  214.5 10.0 custom-call.30
  228.5 41.8 %all-reduce.33.cloned.1.call-done = (f32[128,128]{0,1:T(8,128)}, f32[128,128]{0,1:T(8,128)}) async-done(((f32[128,128]{0,1:T(8,128)}, f32[128,128]{0,1:T(8,128)}), (f32[128,128]{0,1:T(8,128)}, f32[128,128]{0,1:T(8,128)})) %all-reduce.33.cloned.1.call-update) | async-done | bytes 131088 | tf_op jit(solution)/shard_map/psum | solution.py:12
  273.0 11.7 cholesky.353
  286.1 9.8 custom-call.31
  298.9 11.7 cholesky.265
  311.9 9.8 custom-call.23
  323.9 24.3 %all_gather.31 = bf16[1536,128]{0,1:T(8,128)(2,1)S(1)} all-gather(bf16[768,128]{0,1:T(8,128)(2,1)S(1)} %collective-permute-done.1), channel_id=1, replica_groups=mesh['batch'=1,'row'=2,'col'=4] {'row'}, dimensions={0}, use_global_device_ids=true | all-gather | bytes 589824 | tf_op jit(solution)/shard_map/all_gather | solution.py:36
  348.2 8.0 convolution_bitcast_fusion.7
  356.2 29.7 %convolution_bitcast_fusion.3 = f32[8192,128]{0,1:T(8,128)} fusion(bf16[4096,128]{0,1:T(8,128)(2,1)} %all-gather.8.cloned.1.call-done, bf16[8192,4096]{1,0:T(8,128)(2,1)} %param.11), kind=kOutput, calls=%fused_computation.3 | convolution fusion | flops 8589934592 | bytes 72351744 | tf_op jit(solution)/shard_map/dot_general | solution.py:37
  388.0 37.2 %reduce-scatter.23.cloned.1.call-done = f32[2048,128]{0,1:T(8,128)} async-done(((f32[8192,128]{0,1:T(8,128)}), f32[2048,128]{0,1:T(8,128)}) %reduce-scatter.23.cloned.1.call-update) | async-done | bytes 1048592 | tf_op jit(solution)/shard_map/reduce_scatter | solution.py:38
  428.0 42.2 %all-reduce.31.cloned.1.call-done = (f32[128,128]{0,1:T(8,128)}, f32[128,128]{0,1:T(8,128)}) async-done(((f32[128,128]{0,1:T(8,128)}, f32[128,128]{0,1:T(8,128)}), (f32[128,128]{0,1:T(8,128)}, f32[128,128]{0,1:T(8,128)})) %all-reduce.31.cloned.1.call-update) | async-done | bytes 131088 | tf_op jit(solution)/shard_map/psum | solution.py:12
  472.0 11.7 cholesky.276
  485.1 9.8 custom-call.24
  499.3 11.7 cholesky.364
  512.4 10.0 custom-call.32
  526.3 41.8 %all-reduce.29.cloned.1.call-done = (f32[128,128]{0,1:T(8,128)}, f32[128,128]{0,1:T(8,128)}) async-done(((f32[128,128]{0,1:T(8,128)}, f32[128,128]{0,1:T(8,128)}), (f32[128,128]{0,1:T(8,128)}, f32[128,128]{0,1:T(8,128)})) %all-reduce.29.cloned.1.call-update) | async-done | bytes 131088 | tf_op jit(solution)/shard_map/psum | solution.py:12
  570.8 11.7 cholesky.375
  583.9 9.8 custom-call.33
  596.7 11.7 cholesky.287
  609.8 9.8 custom-call.25
  621.7 24.3 %all_gather.32 = bf16[1536,128]{0,1:T(8,128)(2,1)S(1)} all-gather(bf16[768,128]{0,1:T(8,128)(2,1)S(1)} %collective-permute-done.2), channel_id=1, replica_groups=mesh['batch'=1,'row'=2,'col'=4] {'row'}, dimensions={0}, use_global_device_ids=true | all-gather | bytes 589824 | tf_op jit(solution)/shard_map/all_gather | solution.py:36
  646.0 7.9 convolution_bitcast_fusion.6
  654.1 29.7 %convolution_bitcast_fusion.2 = f32[8192,128]{0,1:T(8,128)} fusion(bf16[4096,128]{0,1:T(8,128)(2,1)} %all-gather.10.cloned.1.call-done, bf16[8192,4096]{1,0:T(8,128)(2,1)} %param.11), kind=kOutput, calls=%fused_computation.2 | convolution fusion | flops 8589934592 | bytes 72351744 | tf_op jit(solution)/shard_map/dot_general | solution.py:37
  685.9 37.2 %reduce-scatter.25.cloned.1.call-done = f32[2048,128]{0,1:T(8,128)} async-done(((f32[8192,128]{0,1:T(8,128)}), f32[2048,128]{0,1:T(8,128)}) %reduce-scatter.25.cloned.1.call-update) | async-done | bytes 1048592 | tf_op jit(solution)/shard_map/reduce_scatter | solution.py:38
  725.8 42.2 %all-reduce.27.cloned.1.call-done = (f32[128,128]{0,1:T(8,128)}, f32[128,128]{0,1:T(8,128)}) async-done(((f32[128,128]{0,1:T(8,128)}, f32[128,128]{0,1:T(8,128)}), (f32[128,128]{0,1:T(8,128)}, f32[128,128]{0,1:T(8,128)})) %all-reduce.27.cloned.1.call-update) | async-done | bytes 131088 | tf_op jit(solution)/shard_map/psum | solution.py:12
  769.8 11.7 cholesky.298
  782.9 9.8 custom-call.26
  797.1 11.7 cholesky.386
  810.2 10.0 custom-call.34
  824.2 41.8 %all-reduce.25.cloned.1.call-done = (f32[128,128]{0,1:T(8,128)}, f32[128,128]{0,1:T(8,128)}) async-done(((f32[128,128]{0,1:T(8,128)}, f32[128,128]{0,1:T(8,128)}), (f32[128,128]{0,1:T(8,128)}, f32[128,128]{0,1:T(8,128)})) %all-reduce.25.cloned.1.call-update) | async-done | bytes 131088 | tf_op jit(solution)/shard_map/psum | solution.py:12
  868.7 11.7 cholesky.397
  881.7 9.8 custom-call.35
  894.6 11.7 cholesky.309
  907.6 9.8 custom-call.27
  919.5 24.3 %all_gather.33 = bf16[1536,128]{0,1:T(8,128)(2,1)S(1)} all-gather(bf16[768,128]{0,1:T(8,128)(2,1)S(1)} %collective-permute-done.3), channel_id=1, replica_groups=mesh['batch'=1,'row'=2,'col'=4] {'row'}, dimensions={0}, use_global_device_ids=true | all-gather | bytes 589824 | tf_op jit(solution)/shard_map/all_gather | solution.py:36
  943.9 7.9 convolution_bitcast_fusion.5
  951.9 29.7 %convolution_bitcast_fusion.1 = f32[8192,128]{0,1:T(8,128)} fusion(bf16[4096,128]{0,1:T(8,128)(2,1)} %all-gather.12.cloned.1.call-done, bf16[8192,4096]{1,0:T(8,128)(2,1)} %param.11), kind=kOutput, calls=%fused_computation.1 | convolution fusion | flops 8589934592 | bytes 72351744 | tf_op jit(solution)/shard_map/dot_general | solution.py:37
  983.7 37.3 %reduce-scatter.27.cloned.1.call-done = f32[2048,128]{0,1:T(8,128)} async-done(((f32[8192,128]{0,1:T(8,128)}), f32[2048,128]{0,1:T(8,128)}) %reduce-scatter.27.cloned.1.call-update) | async-done | bytes 1048592 | tf_op jit(solution)/shard_map/reduce_scatter | solution.py:38
  1021.0 2.5 fusion.6
  1023.7 42.2 %all-reduce.23.cloned.1.call-done = (f32[128,128]{0,1:T(8,128)}, f32[128,128]{0,1:T(8,128)}) async-done(((f32[128,128]{0,1:T(8,128)}, f32[128,128]{0,1:T(8,128)}), (f32[128,128]{0,1:T(8,128)}, f32[128,128]{0,1:T(8,128)})) %all-reduce.23.cloned.1.call-update) | async-done | bytes 131088 | tf_op jit(solution)/shard_map/psum | solution.py:12
  1067.7 11.7 cholesky.320
  1080.8 9.8 custom-call.28
  1095.0 11.7 cholesky.408
  1108.1 10.0 custom-call.36
  1122.0 41.8 %all-reduce.21.cloned.1.call-done = (f32[128,128]{0,1:T(8,128)}, f32[128,128]{0,1:T(8,128)}) async-done(((f32[128,128]{0,1:T(8,128)}, f32[128,128]{0,1:T(8,128)}), (f32[128,128]{0,1:T(8,128)}, f32[128,128]{0,1:T(8,128)})) %all-reduce.21.cloned.1.call-update) | async-done | bytes 131088 | tf_op jit(solution)/shard_map/psum | solution.py:12
  1166.6 11.7 cholesky.419
  1179.6 9.8 custom-call.37
  1192.3 11.7 cholesky.331
  1205.4 9.8 custom-call.29
  1217.3 24.3 %all_gather.34 = bf16[1536,128]{0,1:T(8,128)(2,1)S(1)} all-gather(bf16[768,128]{0,1:T(8,128)(2,1)S(1)} %collective-permute-done.4), channel_id=1, replica_groups=mesh['batch'=1,'row'=2,'col'=4] {'row'}, dimensions={0}, use_global_device_ids=true | all-gather | bytes 589824 | tf_op jit(solution)/shard_map/all_gather | solution.py:36
  1241.6 7.9 convolution_bitcast_fusion.4
  1249.6 29.7 %convolution_bitcast_fusion = f32[8192,128]{0,1:T(8,128)} fusion(bf16[4096,128]{0,1:T(8,128)(2,1)} %all-gather.14.cloned.1.call-done, bf16[8192,4096]{1,0:T(8,128)(2,1)} %param.11), kind=kOutput, calls=%fused_computation | convolution fusion | flops 8589934592 | bytes 72351744 | tf_op jit(solution)/shard_map/dot_general | solution.py:37
  1281.5 37.2 %reduce-scatter.29.cloned.1.call-done = f32[2048,128]{0,1:T(8,128)} async-done(((f32[8192,128]{0,1:T(8,128)}), f32[2048,128]{0,1:T(8,128)}) %reduce-scatter.29.cloned.1.call-update) | async-done | bytes 1048592 | tf_op jit(solution)/shard_map/reduce_scatter | solution.py:38
  1318.7 2.9 fusion.97
  1323.8 40.2 %all-reduce.19.cloned.1.call-done = (f32[128,128]{0,1:T(8,128)}, f32[128,128]{0,1:T(8,128)}) async-done(((f32[128,128]{0,1:T(8,128)}, f32[128,128]{0,1:T(8,128)}), (f32[128,128]{0,1:T(8,128)}, f32[128,128]{0,1:T(8,128)})) %all-reduce.19.cloned.1.call-update) | async-done | bytes 131088 | tf_op jit(solution)/shard_map/psum | solution.py:12
  (222 shorter events, 119.1 us)
Async XLA Ops:
  8.0 51.4 %all-gather.6.cloned.1.call-start = ((), (), s32[]{:S(2)}) async-start(), calls=%async_computation.15 | async-start | bytes 1572864 | tf_op jit(solution)/shard_map/all_gather | solution.py:36
  9.3 0.7 collective-permute-start.5
  10.0 0.8 copy-start.4
  10.9 78.0 %reduce-scatter.11.cloned.1.call-start = ((), (), s32[]{:S(2)}) async-start(), calls=%async_computation.10 | async-start | bytes 1966080 | tf_op jit(solution)/shard_map/reduce_scatter | solution.py:38
  11.9 0.7 collective-permute-start
  59.4 68.8 %reduce-scatter.21.cloned.1.call-start = ((), (), s32[]{:S(2)}) async-start(), calls=%async_computation.16 | async-start | bytes 5242880 | tf_op jit(solution)/shard_map/reduce_scatter | solution.py:38
  88.8 84.4 %all-reduce.35.cloned.1.call-start = ((), (), s32[]{:S(2)}) async-start(), calls=%async_computation.33 | async-start | bytes 262144 | tf_op jit(solution)/shard_map/psum | solution.py:12
  130.7 139.5 %all-reduce.33.cloned.1.call-start = ((), (), s32[]{:S(2)}) async-start(), calls=%async_computation.32 | async-start | bytes 262144 | tf_op jit(solution)/shard_map/psum | solution.py:12
  228.4 127.8 %all-gather.8.cloned.1.call-start = ((), (), s32[]{:S(2)}) async-start(), calls=%async_computation.17 | async-start | bytes 1572864 | tf_op jit(solution)/shard_map/all_gather | solution.py:36
  296.9 24.8 %collective-permute-start.6 = (bf16[2048,128]{0,1:T(8,128)(2,1)S(1)}, bf16[2048,128]{0,1:T(8,128)(2,1)S(1)}, u32[]{:S(2)}, u32[]{:S(2)}) collective-permute-start(bf16[2048,128]{0,1:T(8,128)(2,1)S(1)} %fusion), channel_id=1, source_target_pairs={{0,0},{1,4},{2,1},{3,5},{4,2},{5,6},{6,3},{7,7}} | collective-permute-start | bytes 1572872 | tf_op jit(solution)/shard_map/ppermute | solution.py:35
  321.8 0.8 copy-start.1
  322.6 63.4 %reduce-scatter.13.cloned.1.call-start = ((), (), s32[]{:S(2)}) async-start(), calls=%async_computation.11 | async-start | bytes 1966080 | tf_op jit(solution)/shard_map/reduce_scatter | solution.py:38
  323.2 0.7 collective-permute-start.1
  356.2 69.1 %reduce-scatter.23.cloned.1.call-start = ((), (), s32[]{:S(2)}) async-start(), calls=%async_computation.18 | async-start | bytes 5242880 | tf_op jit(solution)/shard_map/reduce_scatter | solution.py:38
  385.9 84.3 %all-reduce.31.cloned.1.call-start = ((), (), s32[]{:S(2)}) async-start(), calls=%async_computation.31 | async-start | bytes 262144 | tf_op jit(solution)/shard_map/psum | solution.py:12
  427.7 140.4 %all-reduce.29.cloned.1.call-start = ((), (), s32[]{:S(2)}) async-start(), calls=%async_computation.30 | async-start | bytes 262144 | tf_op jit(solution)/shard_map/psum | solution.py:12
  526.3 127.8 %all-gather.10.cloned.1.call-start = ((), (), s32[]{:S(2)}) async-start(), calls=%async_computation.19 | async-start | bytes 1572864 | tf_op jit(solution)/shard_map/all_gather | solution.py:36
  594.8 24.8 %collective-permute-start.7 = (bf16[2048,128]{0,1:T(8,128)(2,1)S(1)}, bf16[2048,128]{0,1:T(8,128)(2,1)S(1)}, u32[]{:S(2)}, u32[]{:S(2)}) collective-permute-start(bf16[2048,128]{0,1:T(8,128)(2,1)S(1)} %fusion.1), channel_id=1, source_target_pairs={{0,0},{1,4},{2,1},{3,5},{4,2},{5,6},{6,3},{7,7}} | collective-permute-start | bytes 1572872 | tf_op jit(solution)/shard_map/ppermute | solution.py:35
  619.6 0.8 copy-start.2
  620.4 63.4 %reduce-scatter.15.cloned.1.call-start = ((), (), s32[]{:S(2)}) async-start(), calls=%async_computation.12 | async-start | bytes 1966080 | tf_op jit(solution)/shard_map/reduce_scatter | solution.py:38
  621.0 0.7 collective-permute-start.2
  654.0 69.1 %reduce-scatter.25.cloned.1.call-start = ((), (), s32[]{:S(2)}) async-start(), calls=%async_computation.20 | async-start | bytes 5242880 | tf_op jit(solution)/shard_map/reduce_scatter | solution.py:38
  683.7 84.3 %all-reduce.27.cloned.1.call-start = ((), (), s32[]{:S(2)}) async-start(), calls=%async_computation.29 | async-start | bytes 262144 | tf_op jit(solution)/shard_map/psum | solution.py:12
  725.6 140.4 %all-reduce.25.cloned.1.call-start = ((), (), s32[]{:S(2)}) async-start(), calls=%async_computation.28 | async-start | bytes 262144 | tf_op jit(solution)/shard_map/psum | solution.py:12
  824.1 127.8 %all-gather.12.cloned.1.call-start = ((), (), s32[]{:S(2)}) async-start(), calls=%async_computation.21 | async-start | bytes 1572864 | tf_op jit(solution)/shard_map/all_gather | solution.py:36
  892.6 24.8 %collective-permute-start.8 = (bf16[2048,128]{0,1:T(8,128)(2,1)S(1)}, bf16[2048,128]{0,1:T(8,128)(2,1)S(1)}, u32[]{:S(2)}, u32[]{:S(2)}) collective-permute-start(bf16[2048,128]{0,1:T(8,128)(2,1)S(1)} %fusion.2), channel_id=1, source_target_pairs={{0,0},{1,4},{2,1},{3,5},{4,2},{5,6},{6,3},{7,7}} | collective-permute-start | bytes 1572872 | tf_op jit(solution)/shard_map/ppermute | solution.py:35
  917.5 0.8 copy-start.3
  918.3 63.4 %reduce-scatter.17.cloned.1.call-start = ((), (), s32[]{:S(2)}) async-start(), calls=%async_computation.13 | async-start | bytes 1966080 | tf_op jit(solution)/shard_map/reduce_scatter | solution.py:38
  918.9 0.7 collective-permute-start.3
  951.8 69.1 %reduce-scatter.27.cloned.1.call-start = ((), (), s32[]{:S(2)}) async-start(), calls=%async_computation.22 | async-start | bytes 5242880 | tf_op jit(solution)/shard_map/reduce_scatter | solution.py:38
  981.6 84.3 %all-reduce.23.cloned.1.call-start = ((), (), s32[]{:S(2)}) async-start(), calls=%async_computation.27 | async-start | bytes 262144 | tf_op jit(solution)/shard_map/psum | solution.py:12
  1023.5 140.4 %all-reduce.21.cloned.1.call-start = ((), (), s32[]{:S(2)}) async-start(), calls=%async_computation.26 | async-start | bytes 262144 | tf_op jit(solution)/shard_map/psum | solution.py:12
  1122.0 127.6 %all-gather.14.cloned.1.call-start = ((), (), s32[]{:S(2)}) async-start(), calls=%async_computation.23 | async-start | bytes 1572864 | tf_op jit(solution)/shard_map/all_gather | solution.py:36
  1190.5 24.7 %collective-permute-start.9 = (bf16[2048,128]{0,1:T(8,128)(2,1)S(1)}, bf16[2048,128]{0,1:T(8,128)(2,1)S(1)}, u32[]{:S(2)}, u32[]{:S(2)}) collective-permute-start(bf16[2048,128]{0,1:T(8,128)(2,1)S(1)} %get-tuple-element.31), channel_id=1, source_target_pairs={{0,0},{1,4},{2,1},{3,5},{4,2},{5,6},{6,3},{7,7}} | collective-permute-start | bytes 1572872 | tf_op jit(solution)/shard_map/ppermute | solution.py:35
  1215.2 0.8 copy-start
  1216.0 63.4 %reduce-scatter.19.cloned.1.call-start = ((), (), s32[]{:S(2)}) async-start(), calls=%async_computation.14 | async-start | bytes 1966080 | tf_op jit(solution)/shard_map/reduce_scatter | solution.py:38
  1216.6 0.7 collective-permute-start.4
  1249.6 69.1 %reduce-scatter.29.cloned.1.call-start = ((), (), s32[]{:S(2)}) async-start(), calls=%async_computation.24 | async-start | bytes 5242880 | tf_op jit(solution)/shard_map/reduce_scatter | solution.py:38
  1279.3 84.7 %all-reduce.19.cloned.1.call-start = ((), (), s32[]{:S(2)}) async-start(), calls=%async_computation.25 | async-start | bytes 262144 | tf_op jit(solution)/shard_map/psum | solution.py:12
Sparse Core Ops, SparseCore 0:
  11.0 41.6 all-gather.5
  130.8 42.2 all-reduce.34
  228.6 41.6 all-reduce.32
  322.7 25.6 all-gather.7
  427.9 42.2 all-reduce.30
  526.4 41.6 all-reduce.28
  620.6 25.6 all-gather.9
  725.7 42.2 all-reduce.26
  824.2 41.6 all-reduce.24
  918.4 25.6 all-gather.11
  1023.6 42.2 all-reduce.22
  1122.1 41.6 all-reduce.20
  1216.1 25.6 all-gather.13
  1321.7 42.2 all-reduce.18
Sparse Core Ops, SparseCore 1:
  59.4 23.3 reduce-scatter.10
  88.9 39.2 reduce-scatter.20
  356.2 23.3 reduce-scatter.12
  386.0 39.2 reduce-scatter.22
  654.1 23.3 reduce-scatter.14
  683.8 39.2 reduce-scatter.24
  951.9 23.3 reduce-scatter.16
  981.7 39.2 reduce-scatter.26
  1249.6 23.3 reduce-scatter.18
  1279.4 39.2 reduce-scatter.28
where the time goes:
time: 1380 us; the launch traced here: 1370 us
  waiting for transfers between devices  563 us (41%)
  other arithmetic  397 us (29%)
  matrix products  243 us (18%)
  blocking collectives  136 us (10%)
  between operations  16.8 us (1%)
    psum x9, waiting for transfers between devices, gram_total(): return lax.psum(local_gram, grid_axes)  376 us
    another operation x48, other arithmetic, cholqr_step(): chol_low = jnp.linalg.cholesky(gram_mat)  198 us
    dot_general x10, matrix products, apply_op(): partial_prod = jnp.dot(op_blk, x_col, preferred_element_type=jnp.float32)  187 us
    reduce_scatter x10, waiting for transfers between devices, apply_op(): lax.psum_scatter(partial_prod, 'col', scatter_dimension=0, tiled=True)  186 us
    another operation x32, other arithmetic, cholqr_step(): lax.linalg.triangular_solve(chol_low, y_mat, left_side=False, lower=True,...  168 us
    all_gather x5, blocking collectives, apply_op(): x_col = lax.all_gather(x_moved, 'row', axis=0, tiled=True)  136 us
    dot_general x18, matrix products, gram_total(): lax.dot_general(lhs_mat, rhs_mat, ROW_CONTRACT, precision=precision, pref...  34 us
  transfers between devices with their start and end apart: 34, of which 14 were waited for; matrix products, arithmetic and copies ran while one was open for 22% of the time, Pallas kernels for 0%

commit v1 on v0

v1 whole, which is shorter than its diff:
```python
import functools

import jax
import jax.numpy as jnp
from jax import lax
from jax.experimental import pallas as pl
from jax.experimental.pallas import tpu as pltpu
from jax.sharding import PartitionSpec as P

SWEEPS = 4
S = 128
RING = 4
HIGH = lax.Precision.HIGHEST
MESH = pl.DeviceIdType.MESH
NT = (((1,), (1,)), ((), ()))


def high_dot(lhs, rhs):
    return jnp.dot(lhs, rhs, precision=HIGH, preferred_element_type=jnp.float32)


def high_dot_nt(lhs, rhs):
    return lax.dot_general(lhs, rhs, NT, precision=HIGH, preferred_element_type=jnp.float32)


def remote(src, dst, send_sem, recv_sem, row, col):
    return pltpu.make_async_remote_copy(
        src_ref=src, dst_ref=dst, send_sem=send_sem, recv_sem=recv_sem,
        device_id={"row": row, "col": col}, device_id_type=MESH,
    )


def inverse_factors(mats):
    lane = lax.broadcasted_iota(jnp.int32, (S, S), 1)
    row = lax.broadcasted_iota(jnp.int32, (S, S), 0)
    lane8 = lax.broadcasted_iota(jnp.int32, (8, S), 1)
    sub8 = lax.broadcasted_iota(jnp.int32, (8, S), 0)

    def panel(p, carry):
        k0 = pl.multiple_of(p * 8, 8)
        for ref in mats:
            full = ref[...]
            rows = ref[pl.ds(k0, 8), :]
            heads = [
                jnp.broadcast_to(jnp.sum(jnp.where(lane8 == k0 + j, rows, 0.0), axis=1, keepdims=True), (8, S))
                for j in range(8)
            ]
            below = jnp.where(row >= k0 + 8, full, 0.0)
            cols = [jnp.sum(jnp.where(lane == k0 + j, below, 0.0), axis=1, keepdims=True) for j in range(8)]
            in_panel8 = (lane8 >= k0) & (lane8 < k0 + 8)
            rows = jnp.where(in_panel8, jnp.where(lane8 - k0 == sub8, 1.0, 0.0), rows)
            done = rows
            for j in range(8):
                piv = heads[j][j : j + 1, :]
                inv = 1.0 / piv
                scaled = rows[j : j + 1, :] * inv
                done = jnp.where(sub8 == j, rows * lax.rsqrt(piv), done)
                mult = jnp.where(sub8 == j, 0.0, heads[j])
                for m in range(j + 1, 8):
                    head_row = heads[m][j : j + 1, :] * inv
                    heads[m] = jnp.where(sub8 == j, head_row, heads[m] - mult * head_row)
                rows = jnp.where(sub8 == j, scaled, rows - mult * scaled)
            rest = jnp.where((lane >= k0) & (lane < k0 + 8) & (row >= k0 + 8), 0.0, full)
            for j in range(8):
                rest = rest - cols[j] * rows[j : j + 1, :]
            ref[...] = rest
            ref[pl.ds(k0, 8), :] = done
        return carry

    lax.fori_loop(0, S // 8, panel, 0)
    for ref in mats:
        ref[...] = jnp.where(lane <= row, ref[...], 0.0)


class Op:
    def __init__(self, **refs):
        self.__dict__.update(refs)


def kernel(
    l_op, l_start, r_op, r_start,
    l_out, l_ray, r_out, r_ray,
    l_a, r_a,
    l_xs, l_xt, l_ps, l_pr, l_y, l_xf,
    r_xs, r_xt, r_ps, r_pr, r_y, r_xf,
    g_loc, g_one, g_sum, g_two, g_tot, l_m, r_m,
    l_asem, r_asem,
    gs_sem, gr_sem, fs_sem, fr_sem, ps_sem, pr_sem, xs_sem, xr_sem,
    a1s_sem, a1r_sem, a2s_sem, a2r_sem, a3s_sem, a3r_sem,
):
    y = lax.axis_index("row")
    col = lax.axis_index("col")
    x = col // 2
    k = col % 2
    mate = x * 2 + (1 - k)

    ops = [
        Op(i=0, n=l_op.shape[0] * 2, start=l_start, out=l_out, ray=l_ray, xs=l_xs, xt=l_xt, ps=l_ps, pr=l_pr, y=l_y, xf=l_xf, m=l_m),
        Op(i=1, n=r_op.shape[0] * 2, start=r_start, out=r_out, ray=r_ray, xs=r_xs, xt=r_xt, ps=r_ps, pr=r_pr, y=r_y, xf=r_xf, m=r_m),
    ]
    for o in ops:
        o.nb = o.n // 8
        o.tiles, o.tn = o.ps.shape[0], o.ps.shape[2]

    l_load = pltpu.make_async_copy(l_op, l_a, l_asem)
    l_load.start()

    def r_tile_col(t):
        half = jnp.where(t < 4, 1 - y, y)
        return pl.multiple_of(half * ops[1].nb + (t % 4) * ops[1].tn, ops[1].tn)

    def r_fetch(t):
        return pltpu.make_async_copy(
            r_op.at[:, pl.ds(r_tile_col(t), ops[1].tn)], r_a.at[t % RING], r_asem.at[t % RING]
        )

    for t in range(RING):
        r_fetch(t).start()

    def gather_start(o, dest_row, my_slot):
        for a in range(2):
            is_self = (dest_row == y) & (x == a)

            @pl.when(is_self)
            def _():
                o.xt[my_slot] = o.xs[...]

            @pl.when(jnp.logical_not(is_self))
            def _():
                remote(o.xs, o.xt.at[my_slot], gs_sem.at[o.i, a], gr_sem.at[o.i, o.src], dest_row, 2 * a + k).start()

    def gather(first):
        for o in ops:
            o.src = x if first else y
            my_slot = 2 * x + k if first else 2 * k + y
            gather_start(o, y if first else x, my_slot)
        for o in ops:
            for a in range(2):
                slot = 2 * a + k if first else 2 * k + a
                from_self = (x == a) if first else ((x == y) & (y == a))

                @pl.when(jnp.logical_not(from_self))
                def _():
                    remote(o.xs, o.xt.at[slot], gs_sem.at[o.i, 0], gr_sem.at[o.i, a], y, col).wait_recv()

                remote(o.xt.at[slot], o.xt.at[slot], fs_sem.at[o.i, a], fr_sem.at[o.i, a], y, mate).start()
        for o in ops:
            for a in range(2):
                slot = 2 * a + k if first else 2 * k + a
                other = 2 * a + (1 - k) if first else 2 * (1 - k) + a
                remote(o.xt.at[slot], o.xt.at[slot], fs_sem.at[o.i, a], fr_sem.at[o.i, a], y, mate).wait_send()
                remote(o.xt.at[other], o.xt.at[other], fs_sem.at[o.i, a], fr_sem.at[o.i, a], y, mate).wait_recv()
                dest_row = y if first else x
                is_self = (dest_row == y) & (x == a)

                @pl.when(jnp.logical_not(is_self))
                def _():
                    remote(o.xs, o.xt.at[slot], gs_sem.at[o.i, a], gr_sem.at[o.i, a], y, col).wait_send()

    def tile_send(o, t):
        return remote(o.ps.at[t], o.pr.at[t], ps_sem.at[o.i, t], pr_sem.at[o.i, t], 1 - y, col)

    def block_dot(o, a_rows):
        total = None
        for s in range(4):
            part = jnp.dot(o.xt[s], a_rows(s), preferred_element_type=jnp.float32)
            total = part if total is None else total + part
        return total

    def multiply_l():
        o = ops[0]
        nb = o.nb
        for t in range(o.tiles):
            start = pl.multiple_of((1 - y) * nb + t * o.tn, 128)
            o.ps[t] = block_dot(o, lambda s: l_a[pl.ds(s * nb, nb), pl.ds(start, o.tn)])
            tile_send(o, t).start()
        for t in range(o.tiles):
            start = pl.multiple_of(y * nb + t * o.tn, 128)
            o.y[:, pl.ds(t * o.tn, o.tn)] = block_dot(o, lambda s: l_a[pl.ds(s * nb, nb), pl.ds(start, o.tn)])

    def multiply_r(last):
        o = ops[1]

        def one(t, carry):
            r_fetch(t).wait()
            b = t % RING
            res = block_dot(o, lambda s: r_a[b, pl.ds(s * o.nb, o.nb), :])

            @pl.when(t < o.tiles)
            def _():
                o.ps[t] = res
                tile_send(o, t).start()

            @pl.when(t >= o.tiles)
            def _():
                o.y[:, pl.ds(pl.multiple_of((t - o.tiles) * o.tn, o.tn), o.tn)] = res

            ahead = t + RING
            if last:

                @pl.when(ahead < 2 * o.tiles)
                def _():
                    r_fetch(ahead).start()
            else:
                r_fetch(lax.rem(ahead, 2 * o.tiles)).start()
            return carry

        lax.fori_loop(0, 2 * o.tiles, one, 0)

    def reduce_finish(o):
        for t in range(o.tiles):
            copy = tile_send(o, t)
            copy.wait_recv()
            o.y[:, t * o.tn : (t + 1) * o.tn] = o.y[:, t * o.tn : (t + 1) * o.tn] + o.pr[t]
        for t in range(o.tiles):
            tile_send(o, t).wait_send()

    def all_reduce(par):
        half, other = pl.ds(pl.multiple_of(k * 64, 64), 64), pl.ds(pl.multiple_of((1 - k) * 64, 64), 64)
        one = remote(g_loc.at[:, other], g_one.at[par], a1s_sem.at[par], a1r_sem.at[par], y, mate)
        one.start()
        one.wait_recv()
        g_sum[...] = g_loc[:, half, :] + g_one[par]
        twos = []
        for q in range(3):
            yd = y + ((q + 1) // 2) * (1 - 2 * y)
            xd = x + ((q + 1) % 2) * (1 - 2 * x)
            two = remote(g_sum, g_two.at[par, q], a2s_sem.at[par, q], a2r_sem.at[par, q], yd, 2 * xd + k)
            two.start()
            twos.append(two)
        for two in twos:
            two.wait_recv()
        g_tot[:, half, :] = (g_sum[...] + g_two[par, 0]) + (g_two[par, 1] + g_two[par, 2])
        three = remote(g_tot.at[:, half], g_tot.at[:, half], a3s_sem.at[par], a3r_sem.at[par], y, mate)
        three.start()
        remote(g_tot.at[:, other], g_tot.at[:, other], a3s_sem.at[par], a3r_sem.at[par], y, mate).wait_recv()
        one.wait_send()
        for two in twos:
            two.wait_send()
        three.wait_send()

    def factor_and_apply():
        for o in ops:
            o.m[...] = g_tot[o.i] / float(o.n)
        inverse_factors([o.m for o in ops])
        for o in ops:
            o.y[...] = high_dot(o.m[...], o.y[...])

    def multiply(last):
        multiply_l()
        multiply_r(last)
        for o in ops:
            reduce_finish(o)

    for o in ops:
        for b in range(o.nb // S):
            o.xs[:, b * S : (b + 1) * S] = o.start[b * S : (b + 1) * S, :].T.astype(jnp.bfloat16)
    gather(True)
    l_load.wait()

    def sweep(i, carry):
        multiply(False)
        for o in ops:
            half = o.y[...].astype(jnp.bfloat16)
            g_loc[o.i] = lax.dot_general(half, half, NT, preferred_element_type=jnp.float32)
        all_reduce(0)
        factor_and_apply()
        for o in ops:
            g_loc[o.i] = high_dot_nt(o.y[...], o.y[...])
        all_reduce(1)
        factor_and_apply()
        for o in ops:
            o.xs[...] = o.y[...].astype(jnp.bfloat16)
        gather(False)
        return carry

    lax.fori_loop(0, SWEEPS, sweep, 0)

    stays = (x == y) & (col == 2 * k + y)
    for o in ops:

        @pl.when(stays)
        def _():
            o.xf[1] = o.y[...]

        @pl.when(jnp.logical_not(stays))
        def _():
            o.xf[0] = o.y[...]
            remote(o.xf.at[0], o.xf.at[1], xs_sem.at[o.i], xr_sem.at[o.i], x, 2 * k + y).start()

    multiply(True)
    for o in ops:
        @pl.when(stays)
        def _():
            g_loc[o.i] = high_dot_nt(o.xf[1], o.y[...])

        @pl.when(jnp.logical_not(stays))
        def _():
            g_loc[o.i] = high_dot_nt(o.xf[0], o.y[...])

    all_reduce(0)
    for o in ops:
        o.ray[...] = g_tot[o.i] / float(o.n)

        @pl.when(jnp.logical_not(stays))
        def _():
            copy = remote(o.xf.at[0], o.xf.at[1], xs_sem.at[o.i], xr_sem.at[o.i], x, 2 * k + y)
            copy.wait_recv()
            copy.wait_send()

        for b in range(o.nb // S):
            o.out[b * S : (b + 1) * S, :] = o.xf[1, :, b * S : (b + 1) * S].T


def solution(mesh):
    def local_program(left_op, left_start, right_op, right_start):
        def blocks(n, tiles):
            nb = n // 8
            f32, bf16 = jnp.float32, jnp.bfloat16
            return [
                pltpu.VMEM((S, nb), bf16),
                pltpu.VMEM((4, S, nb), bf16),
                pltpu.VMEM((tiles, S, nb // tiles), f32),
                pltpu.VMEM((tiles, S, nb // tiles), f32),
                pltpu.VMEM((S, nb), f32),
                pltpu.VMEM((2, S, nb), f32),
            ]

        l_n, r_n = left_op.shape[0] * 2, right_op.shape[0] * 2
        f32 = jnp.float32
        dma = pltpu.SemaphoreType.DMA
        vmem = pl.BlockSpec(memory_space=pltpu.VMEM)
        hbm = pl.BlockSpec(memory_space=pl.ANY)
        left_basis, left_ray, right_basis, right_ray = pl.pallas_call(
            kernel,
            out_shape=(
                jax.ShapeDtypeStruct((l_n // 8, S), f32),
                jax.ShapeDtypeStruct((S, S), f32),
                jax.ShapeDtypeStruct((r_n // 8, S), f32),
                jax.ShapeDtypeStruct((S, S), f32),
            ),
            in_specs=[hbm, vmem, hbm, vmem],
            out_specs=(vmem, vmem, vmem, vmem),
            scratch_shapes=[
                pltpu.VMEM(left_op.shape, jnp.bfloat16),
                pltpu.VMEM((RING, right_op.shape[0], r_n // 8 // 4), jnp.bfloat16),
                *blocks(l_n, 1),
                *blocks(r_n, 4),
                pltpu.VMEM((2, S, S), f32),
                pltpu.VMEM((2, 2, 64, S), f32),
                pltpu.VMEM((2, 64, S), f32),
                pltpu.VMEM((2, 3, 2, 64, S), f32),
                pltpu.VMEM((2, S, S), f32),
                pltpu.VMEM((S, S), f32),
                pltpu.VMEM((S, S), f32),
                dma,
                dma((RING,)),
                dma((2, 2)), dma((2, 2)), dma((2, 2)), dma((2, 2)),
                dma((2, 4)), dma((2, 4)), dma((2,)), dma((2,)),
                dma((2,)), dma((2,)), dma((2, 3)), dma((2, 3)), dma((2,)), dma((2,)),
            ],
            compiler_params=pltpu.CompilerParams(has_side_effects=True, vmem_limit_bytes=64 * 1024 * 1024 - 65536),
        )(left_op, left_start, right_op, right_start)
        return left_basis, left_ray, right_basis, right_ray

    op_spec = P(("batch", "row"), "col")
    vec_spec = P(("batch", "row", "col"), None)
    small_spec = P("batch", None)
    return jax.shard_map(
        local_program, mesh=mesh, in_specs=(op_spec, vec_spec, op_spec, vec_spec),
        out_specs=(vec_spec, small_spec, vec_spec, small_spec), check_vma=False,
    )
```

time: 1380 us -> 440 us (0.32)
  waiting for transfers between devices: 563 us -> 0 us
  Pallas kernels: 0 us -> 432 us
  other arithmetic: 397 us -> 0 us
  matrix products: 243 us -> 0 us
  blocking collectives: 136 us -> 0 us
  between operations: 16.8 us -> 0.64 us
    pallas_call x0 -> x1, Pallas kernels: none -> 432 us  [local_program(): pl.pallas_call(kernel, out_shape=(jax.ShapeDtypeStruct((l_n // 8, S), f32...]
    psum x9 -> x0, waiting for transfers between devices: 376 us -> none  [gram_total(): return lax.psum(local_gram, grid_axes)]
    another operation x80 -> x0, other arithmetic: 366 us -> none  [the longest x48 198 us: cholqr_step(): chol_low = jnp.linalg.cholesky(gram_mat)]
    dot_general x28 -> x0, matrix products: 221 us -> none  [the longest x10 187 us: apply_op(): partial_prod = jnp.dot(op_blk, x_col, preferred_element_type=jnp.float32)]
    reduce_scatter x10 -> x0, waiting for transfers between devices: 186 us -> none  [apply_op(): lax.psum_scatter(partial_prod, 'col', scatter_dimension=0, tiled=True)]
    all_gather x5 -> x0, blocking collectives: 136 us -> none  [apply_op(): x_col = lax.all_gather(x_moved, 'row', axis=0, tiled=True)]
    div x33 -> x0, other arithmetic: 28.1 us -> none  [the longest x15 12.9 us: cholqr_step(): chol_low = jnp.linalg.cholesky(gram_mat)]
    another operation x16 -> x0, matrix products: 21.4 us -> none  [cholqr_step(): lax.linalg.triangular_solve(chol_low, y_mat, left_side=False, lower=True,...]
  transfers between devices with their start and end apart: 34 -> 0, of which waited for: 14 -> 0; matrix products, arithmetic and copies ran while one was open for 22% -> 0% of each run, Pallas kernels for 0% -> 0%
where the time goes in v1:
time: 440 us
  Pallas kernels  432 us (98%)
  local copies, waits for them, and re-layouts  6.97 us (2%)
    pallas_call x1, Pallas kernels, local_program(): pl.pallas_call(kernel, out_shape=(jax.ShapeDtypeStruct((l_n // 8, S), f32...  432 us

profile of v1, /device:TPU:0, one launch (start us, length us, event | category | flops | bytes accessed | tf_op | source)
XLA Modules:
  0.0 439.5 jit_solution(7422468614447921923)
XLA Ops:
  0.6 431.9 %shard_map.75 = (f32[768,128]{1,0:T(8,128)}, f32[128,128]{1,0:T(8,128)}, f32[2048,128]{1,0:T(8,128)}, f32[128,128]{1,0:T(8,128)}) custom-call(bf16[3072,1536]{1,0:T(8,128)(2,1)} %l_op.1, f32[768,128]{1,0:T(8,128)} %l_start.1, bf16[8192,4096]{1,0:T(8,128)(2,1)} %r_op.1, f32[2048,128]{1,0:T(8,128)} %r_start.1), custom_call_target="tpu_custom_call" | custom-call | tf_op jit(solution)/shard_map/pallas_call | solution.py:334
  432.5 1.8 copy.12
  434.3 1.5 copy.13
  435.8 2.3 copy.14
  438.0 1.5 copy.15

commit v2 on v0

v2 whole, which is shorter than its diff:
```python
import jax
import jax.numpy as jnp
from jax import lax
from jax.experimental import pallas as pl
from jax.experimental.pallas import tpu as pltpu
from jax.sharding import PartitionSpec as P

SWEEPS = 4
S = 128
RING = 4
TILES = 4
CHUNKS = 2
PANEL = 16
MESH = pl.DeviceIdType.MESH
F32, BF16 = jnp.float32, jnp.bfloat16
NT = (((1,), (1,)), ((), ()))
TN = (((0,), (0,)), ((), ()))


def dot(lhs, rhs):
    return jnp.dot(lhs, rhs, preferred_element_type=F32)


def dot_nt(lhs, rhs):
    return lax.dot_general(lhs, rhs, NT, preferred_element_type=F32)


def split(value):
    high = value.astype(BF16)
    rest = value - high.astype(F32)
    mid = rest.astype(BF16)
    low = (rest - mid.astype(F32)).astype(BF16)
    return high, mid, low


def remote(src, dst, send_sem, recv_sem, row, col):
    return pltpu.make_async_remote_copy(
        src_ref=src, dst_ref=dst, send_sem=send_sem, recv_sem=recv_sem,
        device_id={"row": row, "col": col}, device_id_type=MESH,
    )


def inverse_factors(mats):
    sub = lax.broadcasted_iota(jnp.int32, (PANEL, S), 0)
    lane = lax.broadcasted_iota(jnp.int32, (PANEL, S), 1)

    tall_row = lax.broadcasted_iota(jnp.int32, (S, S), 0)
    tall_lane = lax.broadcasted_iota(jnp.int32, (S, S), 1)

    def panel(p, carry):
        k0 = pl.multiple_of(p * PANEL, PANEL)
        inside = (tall_lane >= k0) & (tall_lane < k0 + PANEL) & (tall_row >= k0 + PANEL)
        at = lane - k0
        for ref in mats:
            rows = ref[pl.ds(k0, PANEL), :]
            heads = jnp.stack(
                [
                    jnp.broadcast_to(jnp.sum(jnp.where(at == j, rows, 0.0), axis=1, keepdims=True), (PANEL, S))
                    for j in range(PANEL)
                ]
            )
            high, mid, low = split(jnp.where(at >= PANEL, rows, 0.0))
            cols = jnp.concatenate([high, mid, high, mid, high, low], axis=0)
            rows = jnp.where((at >= 0) & (at < PANEL), jnp.where(at == sub, 1.0, 0.0), rows)
            done = rows
            piv = heads[0, 0:1, :]
            for j in range(PANEL):
                here = sub == j
                root = lax.rsqrt(piv)
                inv = root * root
                done = jnp.where(here, rows * root, done)
                mult = jnp.where(here, 0.0, heads[0])
                if j < PANEL - 1:
                    head_rows = heads[1:, j : j + 1, :] * inv
                    piv = heads[1, j + 1 : j + 2, :] - heads[0, j + 1 : j + 2, :] * head_rows[0]
                    heads = jnp.where(here[None], head_rows, heads[1:] - mult[None] * head_rows)
                scaled = rows[j : j + 1, :] * inv
                rows = jnp.where(here, scaled, rows - mult * scaled)
            high, mid, low = split(rows)
            rhs = jnp.concatenate([high, high, mid, mid, low, high], axis=0)
            change = lax.dot_general(cols, rhs, TN, preferred_element_type=F32)
            ref[...] = jnp.where(inside, 0.0, ref[...]) - change
            ref[pl.ds(k0, PANEL), :] = done
        return carry

    lax.fori_loop(0, S // PANEL, panel, 0)
    for ref in mats:
        ref[...] = jnp.where(tall_lane <= tall_row, ref[...], 0.0)


class Op:
    def __init__(self, **refs):
        self.__dict__.update(refs)


def kernel(
    l_op, l_start, r_op, r_start,
    l_out, r_out, ray_out,
    l_a, r_a,
    l_xs, l_xt, l_mate_s, l_mate_r, l_side_s, l_side_r, l_y, l_m, l_sp,
    r_xs, r_xt, r_ps, r_pr, r_y, r_m, r_sp, r_keep,
    g_loc, g_one, g_sum, g_two, g_tot,
    l_asem, r_asem,
    gs_sem, gr_sem, fs_sem, fr_sem, ps_sem, pr_sem, xs_sem, xr_sem,
    lgs_sem, lgr_sem, lms_sem, lmr_sem, lss_sem, lsr_sem,
    a1s_sem, a1r_sem, a2s_sem, a2r_sem, a3s_sem, a3r_sem,
):
    y = lax.axis_index("row")
    col = lax.axis_index("col")
    x = col // 2
    k = col % 2
    mate = x * 2 + (1 - k)
    l_n, r_n = l_op.shape[0] * 2, r_op.shape[0] * 2
    l_nb, r_nb = l_n // 8, r_n // 8
    tile = r_nb // TILES
    piece = r_nb // CHUNKS

    left = Op(i=0, n=l_n, nb=l_nb, y=l_y, m=l_m, sp=l_sp)
    right = Op(i=1, n=r_n, nb=r_nb, y=r_y, m=r_m, sp=r_sp)
    ops = [left, right]

    l_load = pltpu.make_async_copy(l_op, l_a, l_asem)
    l_load.start()

    def r_fetch(t):
        half = jnp.where(t < TILES, 1 - y, y)
        start = pl.multiple_of(half * r_nb + (t % TILES) * tile, tile)
        return pltpu.make_async_copy(r_op.at[:, pl.ds(start, tile)], r_a.at[t % RING], r_asem.at[t % RING])

    for t in range(RING):
        r_fetch(t).start()

    class Gather:
        def __init__(self, first):
            self.dest_row = y if first else x
            self.my_slot = 2 * x + k if first else 2 * k + y
            self.src = x if first else y
            self.slots = [2 * a + k if first else 2 * k + a for a in range(2)]
            self.other_slots = [2 * a + (1 - k) if first else 2 * (1 - k) + a for a in range(2)]
            self.sends_to_self = [(self.dest_row == y) & (x == a) for a in range(2)]
            self.gets_from_self = [(x == a) if first else ((x == y) & (y == a)) for a in range(2)]

        def copy(self, a, h, recv):
            return remote(
                r_xs.at[h], r_xt.at[self.my_slot, h], gs_sem.at[a, h], gr_sem.at[recv, h], self.dest_row, 2 * a + k
            )

        def forward(self, a, h, slots):
            ref = r_xt.at[slots[a], h]
            return remote(ref, ref, fs_sem.at[a, h], fr_sem.at[a, h], y, mate)

        def start(self, h):
            for a in range(2):

                @pl.when(self.sends_to_self[a])
                def _():
                    r_xt[self.my_slot, h] = r_xs[h]

                @pl.when(jnp.logical_not(self.sends_to_self[a]))
                def _():
                    self.copy(a, h, self.src).start()

        def finish(self):
            for h in range(CHUNKS):
                for a in range(2):

                    @pl.when(jnp.logical_not(self.gets_from_self[a]))
                    def _():
                        self.copy(0, h, a).wait_recv()

                    self.forward(a, h, self.slots).start()
            for h in range(CHUNKS):
                for a in range(2):
                    self.forward(a, h, self.other_slots).wait_recv()

        def drain(self):
            for h in range(CHUNKS):
                for a in range(2):
                    self.forward(a, h, self.slots).wait_send()

                    @pl.when(jnp.logical_not(self.sends_to_self[a]))
                    def _():
                        self.copy(a, h, self.src).wait_send()

    def left_copy(b, slot):
        return remote(l_xs, l_xt.at[slot], lgs_sem.at[b], lgr_sem.at[slot], b, 2 * y + x)

    def left_self(b):
        return (b == y) & (y == x) & (x == k)

    def left_start():
        for b in range(2):

            @pl.when(left_self(b))
            def _():
                l_xt[k] = l_xs[...]

            @pl.when(jnp.logical_not(left_self(b)))
            def _():
                left_copy(b, k).start()

    def left_finish():
        for slot in range(2):

            @pl.when(jnp.logical_not((y == x) & (x == k) & (k == slot)))
            def _():
                left_copy(0, slot).wait_recv()

    def left_drain():
        for b in range(2):

            @pl.when(jnp.logical_not(left_self(b)))
            def _():
                left_copy(b, k).wait_send()

    def left_block(index):
        rows = pl.ds(pl.multiple_of(index * l_nb, l_nb), l_nb)
        return dot_nt(l_xt[0], l_a[rows, :l_nb]) + dot_nt(l_xt[1], l_a[rows, l_nb:])

    def left_mate(a):
        return remote(l_mate_s.at[a], l_mate_r.at[a], lms_sem.at[a], lmr_sem.at[a], y, mate)

    def left_side():
        return remote(l_side_s, l_side_r, lss_sem, lsr_sem, y, 2 * (1 - x) + k)

    def left_multiply():
        for a in (1 - x, x):
            l_mate_s[a] = left_block(2 * a + (1 - k))
            left_mate(a).start()
        l_side_s[...] = left_block(2 * (1 - x) + k)
        l_y[...] = left_block(2 * x + k)

    def left_reduce_start():
        left_mate(1 - x).wait_recv()
        l_side_s[...] = l_side_s[...] + l_mate_r[1 - x]
        left_side().start()
        left_mate(x).wait_recv()
        l_y[...] = l_y[...] + l_mate_r[x]

    def left_reduce_finish():
        left_side().wait_recv()
        l_y[...] = l_y[...] + l_side_r[...]
        left_side().wait_send()
        for a in range(2):
            left_mate(a).wait_send()

    def right_send(t):
        return remote(r_ps.at[t], r_pr.at[t], ps_sem.at[t], pr_sem.at[t], 1 - y, col)

    def right_tile(t):
        r_fetch(t).wait()
        b = t % RING
        total = None
        for s in range(4):
            for h in range(CHUNKS):
                part = dot(r_xt[s, h], r_a[b, s * r_nb + h * piece : s * r_nb + (h + 1) * piece, :])
                total = part if total is None else total + part
        return total

    def right_multiply(own, last):
        def one(i, carry):
            t = i + TILES * own
            res = right_tile(t)
            if own:
                r_y[:, pl.ds(pl.multiple_of(i * tile, tile), tile)] = res
            else:
                r_ps[i] = res
                right_send(i).start()
            ahead = t + RING
            if not (last and own):
                r_fetch(lax.rem(ahead, 2 * TILES)).start()
            return carry

        lax.fori_loop(0, TILES, one, 0)

    def right_reduce_finish():
        for t in range(TILES):
            right_send(t).wait_recv()
            r_y[:, t * tile : (t + 1) * tile] = r_y[:, t * tile : (t + 1) * tile] + r_pr[t]
        for t in range(TILES):
            right_send(t).wait_send()

    def all_reduce(par):
        half, other = pl.ds(pl.multiple_of(k * 64, 64), 64), pl.ds(pl.multiple_of((1 - k) * 64, 64), 64)
        one = remote(g_loc.at[:, other], g_one.at[par], a1s_sem.at[par], a1r_sem.at[par], y, mate)
        one.start()
        one.wait_recv()
        g_sum[...] = g_loc[:, half, :] + g_one[par]
        twos = []
        for q in (2, 1, 0):
            yd = y + ((q + 1) // 2) * (1 - 2 * y)
            xd = x + ((q + 1) % 2) * (1 - 2 * x)
            two = remote(g_sum, g_two.at[par, q], a2s_sem.at[par, q], a2r_sem.at[par, q], yd, 2 * xd + k)
            two.start()
            twos.append(two)
        for two in twos:
            two.wait_recv()
        g_tot[:, half, :] = (g_sum[...] + g_two[par, 0]) + (g_two[par, 1] + g_two[par, 2])
        three = remote(g_tot.at[:, half], g_tot.at[:, half], a3s_sem.at[par], a3r_sem.at[par], y, mate)
        three.start()
        remote(g_tot.at[:, other], g_tot.at[:, other], a3s_sem.at[par], a3r_sem.at[par], y, mate).wait_recv()
        one.wait_send()
        for two in twos:
            two.wait_send()
        three.wait_send()

    def factor():
        for o in ops:
            o.m[...] = g_tot[o.i] / float(o.n)
        inverse_factors([o.m for o in ops])

    def apply_piece(o, lhs, start, width):
        high, mid, low = split(o.y[:, start : start + width])
        rhs = jnp.concatenate([high, high, mid, mid, low, high], axis=0)
        return dot(lhs, rhs)

    def apply_lhs(o):
        high, mid, low = split(o.m[...])
        return jnp.concatenate([high, mid, high, mid, high, low], axis=1)

    def second_gram(o):
        lhs = apply_lhs(o)
        for start in range(0, o.nb, 256):
            res = apply_piece(o, lhs, start, 256)
            o.y[:, start : start + 256] = res
            parts = split(res)
            for q in range(3):
                o.sp[q * S : (q + 1) * S, start : start + 256] = parts[q]
        both = dot_nt(o.sp[: 2 * S, :], o.sp[: 2 * S, :])
        cross = dot_nt(o.sp[:S, :], o.sp[2 * S :, :])
        g_loc[o.i] = both[:S, :S] + ((both[:S, S:] + both[S:, :S]) + (both[S:, S:] + (cross + cross.T)))

    def rayleigh(o, basis):
        g_loc[o.i] = lax.dot_general(basis, o.y[...], NT, precision=lax.Precision.HIGHEST, preferred_element_type=F32)

    def new_basis(gather):
        lhs = apply_lhs(right)
        for h in range(CHUNKS):
            for start in range(h * piece, (h + 1) * piece, 256):
                res = apply_piece(right, lhs, start, 256)
                r_y[:, start : start + 256] = res
                r_xs[h, :, start - h * piece : start - h * piece + 256] = res.astype(BF16)
            gather.start(h)
        lhs = apply_lhs(left)
        for start in range(0, l_nb, 256):
            res = apply_piece(left, lhs, start, 256)
            l_y[:, start : start + 256] = res
            l_xs[:, start : start + 256] = res.astype(BF16)
        left_start()

    def multiply(gather, last):
        gather.finish()
        right_multiply(0, last)
        left_finish()
        left_multiply()
        right_multiply(1, last)
        left_reduce_start()
        right_reduce_finish()
        left_reduce_finish()
        gather.drain()
        left_drain()

    first, later = Gather(True), Gather(False)
    for h in range(CHUNKS):
        for b in range(piece // S):
            r_xs[h, :, b * S : (b + 1) * S] = r_start[h * piece + b * S : h * piece + (b + 1) * S, :].T.astype(BF16)
        first.start(h)
    for b in range(l_nb // S):
        l_xs[:, b * S : (b + 1) * S] = l_start[b * S : (b + 1) * S, :].T.astype(BF16)
    left_start()
    first.finish()
    first.drain()
    l_load.wait()

    class Ready:
        def finish(self):
            pass

        def drain(self):
            pass

    def sweep(i, carry):
        multiply(Ready(), False)
        for o in ops:
            half = o.y[...].astype(BF16)
            g_loc[o.i] = dot_nt(half, half)
        all_reduce(0)
        factor()
        for o in ops:
            second_gram(o)
        all_reduce(1)
        factor()
        new_basis(later)
        later.finish()
        later.drain()
        return carry

    lax.fori_loop(0, SWEEPS, sweep, 0)

    stays = (x == y) & (col == 2 * k + y)
    home = remote(r_keep.at[0], r_keep.at[1], xs_sem, xr_sem, x, 2 * k + y)
    r_keep[0] = r_y[...]

    @pl.when(stays)
    def _():
        r_keep[1] = r_y[...]

    @pl.when(jnp.logical_not(stays))
    def _():
        home.start()

    l_out[...] = l_y[...]
    multiply(Ready(), True)
    rayleigh(left, l_out[...])
    rayleigh(right, r_keep[0])
    all_reduce(0)
    for o in ops:
        ray_out[o.i] = g_tot[o.i] / float(o.n)

    @pl.when(jnp.logical_not(stays))
    def _():
        home.wait_recv()
        home.wait_send()

    r_out[...] = r_keep[1]


def finish_kernel(l_in, r_in, ray_in, l_out, l_ray, r_out, r_ray):
    for src, dst in ((l_in, l_out), (r_in, r_out)):
        for b in range(dst.shape[0] // S):
            dst[b * S : (b + 1) * S, :] = src[:, b * S : (b + 1) * S].T
    l_ray[...] = ray_in[0]
    r_ray[...] = ray_in[1]


def solution(mesh):
    def local_program(left_op, left_start, right_op, right_start):
        l_nb, r_nb = left_op.shape[0] // 4, right_op.shape[0] // 4
        dma = pltpu.SemaphoreType.DMA
        vmem = pl.BlockSpec(memory_space=pltpu.VMEM)
        hbm = pl.BlockSpec(memory_space=pl.ANY)
        shape = jax.ShapeDtypeStruct
        left_t, right_t, rayleigh = pl.pallas_call(
            kernel,
            out_shape=(shape((S, l_nb), F32), shape((S, r_nb), F32), shape((2, S, S), F32)),
            in_specs=[hbm, vmem, hbm, vmem],
            out_specs=(vmem, vmem, vmem),
            scratch_shapes=[
                pltpu.VMEM(left_op.shape, BF16),
                pltpu.VMEM((RING, right_op.shape[0], r_nb // TILES), BF16),
                pltpu.VMEM((S, l_nb), BF16),
                pltpu.VMEM((2, S, l_nb), BF16),
                pltpu.VMEM((2, S, l_nb), F32),
                pltpu.VMEM((2, S, l_nb), F32),
                pltpu.VMEM((S, l_nb), F32),
                pltpu.VMEM((S, l_nb), F32),
                pltpu.VMEM((S, l_nb), F32),
                pltpu.VMEM((S, S), F32),
                pltpu.VMEM((3 * S, l_nb), BF16),
                pltpu.VMEM((CHUNKS, S, r_nb // CHUNKS), BF16),
                pltpu.VMEM((4, CHUNKS, S, r_nb // CHUNKS), BF16),
                pltpu.VMEM((TILES, S, r_nb // TILES), F32),
                pltpu.VMEM((TILES, S, r_nb // TILES), F32),
                pltpu.VMEM((S, r_nb), F32),
                pltpu.VMEM((S, S), F32),
                pltpu.VMEM((3 * S, r_nb), BF16),
                pltpu.VMEM((2, S, r_nb), F32),
                pltpu.VMEM((2, S, S), F32),
                pltpu.VMEM((2, 2, 64, S), F32),
                pltpu.VMEM((2, 64, S), F32),
                pltpu.VMEM((2, 3, 2, 64, S), F32),
                pltpu.VMEM((2, S, S), F32),
                dma, dma((RING,)),
                dma((2, CHUNKS)), dma((2, CHUNKS)), dma((2, CHUNKS)), dma((2, CHUNKS)),
                dma((TILES,)), dma((TILES,)), dma, dma,
                dma((2,)), dma((2,)), dma((2,)), dma((2,)), dma, dma,
                dma((2,)), dma((2,)), dma((2, 3)), dma((2, 3)), dma((2,)), dma((2,)),
            ],
            compiler_params=pltpu.CompilerParams(has_side_effects=True, vmem_limit_bytes=64 * 1024 * 1024 - 65536),
        )(left_op, left_start, right_op, right_start)
        left_basis, left_ray, right_basis, right_ray = pl.pallas_call(
            finish_kernel,
            out_shape=(shape((l_nb, S), F32), shape((S, S), F32), shape((r_nb, S), F32), shape((S, S), F32)),
            in_specs=[vmem] * 3,
            out_specs=(vmem,) * 4,
        )(left_t, right_t, rayleigh)
        return left_basis, left_ray, right_basis, right_ray

    op_spec = P(("batch", "row"), "col")
    vec_spec = P(("batch", "row", "col"), None)
    small_spec = P("batch", None)
    return jax.shard_map(
        local_program, mesh=mesh, in_specs=(op_spec, vec_spec, op_spec, vec_spec),
        out_specs=(vec_spec, small_spec, vec_spec, small_spec), check_vma=False,
    )
```

time: 1380 us -> 355 us (0.26)
  waiting for transfers between devices: 563 us -> 0 us
  other arithmetic: 397 us -> 0 us
  Pallas kernels: 0 us -> 354 us
  matrix products: 243 us -> 0 us
  blocking collectives: 136 us -> 0 us
  between operations: 16.8 us -> 0.64 us
    psum x9 -> x0, waiting for transfers between devices: 376 us -> none  [gram_total(): return lax.psum(local_gram, grid_axes)]
    another operation x80 -> x0, other arithmetic: 366 us -> none  [the longest x48 198 us: cholqr_step(): chol_low = jnp.linalg.cholesky(gram_mat)]
    pallas_call x0 -> x2, Pallas kernels: none -> 354 us  [the longest x1 351 us: local_program(): pl.pallas_call(kernel, out_shape=(shape((S, l_nb), F32), shape((S, r_nb),...]
    dot_general x28 -> x0, matrix products: 221 us -> none  [the longest x10 187 us: apply_op(): partial_prod = jnp.dot(op_blk, x_col, preferred_element_type=jnp.float32)]
    reduce_scatter x10 -> x0, waiting for transfers between devices: 186 us -> none  [apply_op(): lax.psum_scatter(partial_prod, 'col', scatter_dimension=0, tiled=True)]
    all_gather x5 -> x0, blocking collectives: 136 us -> none  [apply_op(): x_col = lax.all_gather(x_moved, 'row', axis=0, tiled=True)]
    div x33 -> x0, other arithmetic: 28.1 us -> none  [the longest x15 12.9 us: cholqr_step(): chol_low = jnp.linalg.cholesky(gram_mat)]
    another operation x16 -> x0, matrix products: 21.4 us -> none  [cholqr_step(): lax.linalg.triangular_solve(chol_low, y_mat, left_side=False, lower=True,...]
  transfers between devices with their start and end apart: 34 -> 0, of which waited for: 14 -> 0; matrix products, arithmetic and copies ran while one was open for 22% -> 0% of each run, Pallas kernels for 0% -> 0%
where the time goes in v2:
time: 355 us
  Pallas kernels  354 us (100%)
    pallas_call x1, Pallas kernels, local_program(): pl.pallas_call(kernel, out_shape=(shape((S, l_nb), F32), shape((S, r_nb),...  351 us

profile of v2, /device:TPU:0, one launch (start us, length us, event | category | flops | bytes accessed | tf_op | source)
XLA Modules:
  0.0 354.6 jit_solution(6683192209171899030)
XLA Ops:
  0.6 351.2 %shard_map.75 = (f32[128,768]{1,0:T(8,128)}, f32[128,2048]{1,0:T(8,128)}, f32[2,128,128]{2,1,0:T(8,128)}) custom-call(bf16[3072,1536]{1,0:T(8,128)(2,1)} %l_op.1, f32[768,128]{1,0:T(8,128)} %l_start.1, bf16[8192,4096]{1,0:T(8,128)(2,1)} %r_op.1, f32[2048,128]{1,0:T(8,128)} %r_start.1), custom_call_target="tpu_custom_call" | custom-call | tf_op jit(solution)/shard_map/pallas_call | solution.py:443
  351.8 2.8 shard_map.76

commit v3 on v2

--- a/solution.py
+++ b/solution.py
@@ -9,7 +9,7 @@
 S = 128
 RING = 4
 TILES = 4
-CHUNKS = 2
+CHUNKS = 4
 PANEL = 16
 MESH = pl.DeviceIdType.MESH
 F32, BF16 = jnp.float32, jnp.bfloat16
@@ -98,10 +98,10 @@
     l_out, r_out, ray_out,
     l_a, r_a,
     l_xs, l_xt, l_mate_s, l_mate_r, l_side_s, l_side_r, l_y, l_m, l_sp,
-    r_xs, r_xt, r_ps, r_pr, r_y, r_m, r_sp, r_keep,
+    r_xs, r_xt, r_hand, r_ps, r_pr, r_y, r_m, r_sp, r_keep,
     g_loc, g_one, g_sum, g_two, g_tot,
     l_asem, r_asem,
-    gs_sem, gr_sem, fs_sem, fr_sem, ps_sem, pr_sem, xs_sem, xr_sem,
+    gs_sem, gr_sem, fs_sem, fr_sem, hs_sem, hr_sem, ps_sem, pr_sem, xs_sem, xr_sem,
     lgs_sem, lgr_sem, lms_sem, lmr_sem, lss_sem, lsr_sem,
     a1s_sem, a1r_sem, a2s_sem, a2r_sem, a3s_sem, a3r_sem,
 ):
@@ -139,12 +139,20 @@
             self.other_slots = [2 * a + (1 - k) if first else 2 * (1 - k) + a for a in range(2)]
             self.sends_to_self = [(self.dest_row == y) & (x == a) for a in range(2)]
             self.gets_from_self = [(x == a) if first else ((x == y) & (y == a)) for a in range(2)]
+            self.relays = None if first else x == y
+            self.sends_across = [False if first else (x != y) & (a == y) for a in range(2)]
 
         def copy(self, a, h, recv):
             return remote(
                 r_xs.at[h], r_xt.at[self.my_slot, h], gs_sem.at[a, h], gr_sem.at[recv, h], self.dest_row, 2 * a + k
             )
 
+        def across(self, a, h):
+            return remote(r_xs.at[h], r_hand.at[h], gs_sem.at[a, h], hr_sem.at[h], y, 2 * (1 - x) + k)
+
+        def hand_on(self, h):
+            return remote(r_hand.at[h], r_xt.at[2 * k + y, h], hs_sem.at[h], gr_sem.at[y, h], 1 - y, col)
+
         def forward(self, a, h, slots):
             ref = r_xt.at[slots[a], h]
             return remote(ref, ref, fs_sem.at[a, h], fr_sem.at[a, h], y, mate)
@@ -156,12 +164,25 @@
                 def _():
                     r_xt[self.my_slot, h] = r_xs[h]
 
-                @pl.when(jnp.logical_not(self.sends_to_self[a]))
+                if self.relays is not None:
+
+                    @pl.when(self.sends_across[a])
+                    def _():
+                        self.across(a, h).start()
+
+                @pl.when(jnp.logical_not(self.sends_to_self[a] | self.sends_across[a]))
                 def _():
                     self.copy(a, h, self.src).start()
 
         def finish(self):
             for h in range(CHUNKS):
+                if self.relays is not None:
+
+                    @pl.when(self.relays)
+                    def _():
+                        self.across(0, h).wait_recv()
+                        self.hand_on(h).start()
+
                 for a in range(2):
 
                     @pl.when(jnp.logical_not(self.gets_from_self[a]))
@@ -181,6 +202,12 @@
                     @pl.when(jnp.logical_not(self.sends_to_self[a]))
                     def _():
                         self.copy(a, h, self.src).wait_send()
+
+                if self.relays is not None:
+
+                    @pl.when(self.relays)
+                    def _():
+                        self.hand_on(h).wait_send()
 
     def left_copy(b, slot):
         return remote(l_xs, l_xt.at[slot], lgs_sem.at[b], lgr_sem.at[slot], b, 2 * y + x)
@@ -459,6 +486,7 @@
                 pltpu.VMEM((3 * S, l_nb), BF16),
                 pltpu.VMEM((CHUNKS, S, r_nb // CHUNKS), BF16),
                 pltpu.VMEM((4, CHUNKS, S, r_nb // CHUNKS), BF16),
+                pltpu.VMEM((CHUNKS, S, r_nb // CHUNKS), BF16),
                 pltpu.VMEM((TILES, S, r_nb // TILES), F32),
                 pltpu.VMEM((TILES, S, r_nb // TILES), F32),
                 pltpu.VMEM((S, r_nb), F32),
@@ -471,7 +499,7 @@
                 pltpu.VMEM((2, 3, 2, 64, S), F32),
                 pltpu.VMEM((2, S, S), F32),
                 dma, dma((RING,)),
-                dma((2, CHUNKS)), dma((2, CHUNKS)), dma((2, CHUNKS)), dma((2, CHUNKS)),
+                dma((2, CHUNKS)), dma((2, CHUNKS)), dma((2, CHUNKS)), dma((2, CHUNKS)), dma((CHUNKS,)), dma((CHUNKS,)),
                 dma((TILES,)), dma((TILES,)), dma, dma,
                 dma((2,)), dma((2,)), dma((2,)), dma((2,)), dma, dma,
                 dma((2,)), dma((2,)), dma((2, 3)), dma((2, 3)), dma((2,)), dma((2,)),

time: 355 us -> 374 us (1.054)
  Pallas kernels: 354 us -> 373 us
    pallas_call x1, Pallas kernels: 351 us -> 371 us  [local_program(): pl.pallas_call(kernel, out_shape=(shape((S, l_nb), F32), shape((S, r_nb),...]
where the time goes in v3:
time: 374 us
  Pallas kernels  373 us (100%)
    pallas_call x1, Pallas kernels, local_program(): pl.pallas_call(kernel, out_shape=(shape((S, l_nb), F32), shape((S, r_nb),...  371 us

profile of v3, /device:TPU:0, one launch (start us, length us, event | category | flops | bytes accessed | tf_op | source)
XLA Modules:
  0.0 374.1 jit_solution(7928517137370309162)
XLA Ops:
  0.6 370.7 %shard_map.75 = (f32[128,768]{1,0:T(8,128)}, f32[128,2048]{1,0:T(8,128)}, f32[2,128,128]{2,1,0:T(8,128)}) custom-call(bf16[3072,1536]{1,0:T(8,128)(2,1)} %l_op.1, f32[768,128]{1,0:T(8,128)} %l_start.1, bf16[8192,4096]{1,0:T(8,128)(2,1)} %r_op.1, f32[2048,128]{1,0:T(8,128)} %r_start.1), custom_call_target="tpu_custom_call" | custom-call | tf_op jit(solution)/shard_map/pallas_call | solution.py:470
  371.4 2.8 shard_map.76

commit v4 on v2

--- a/solution.py
+++ b/solution.py
@@ -40,7 +40,7 @@
     )
 
 
-def inverse_factors(mats):
+def inverse_factor(ref):
     sub = lax.broadcasted_iota(jnp.int32, (PANEL, S), 0)
     lane = lax.broadcasted_iota(jnp.int32, (PANEL, S), 1)
 
@@ -51,41 +51,38 @@
         k0 = pl.multiple_of(p * PANEL, PANEL)
         inside = (tall_lane >= k0) & (tall_lane < k0 + PANEL) & (tall_row >= k0 + PANEL)
         at = lane - k0
-        for ref in mats:
-            rows = ref[pl.ds(k0, PANEL), :]
-            heads = jnp.stack(
-                [
-                    jnp.broadcast_to(jnp.sum(jnp.where(at == j, rows, 0.0), axis=1, keepdims=True), (PANEL, S))
-                    for j in range(PANEL)
-                ]
-            )
-            high, mid, low = split(jnp.where(at >= PANEL, rows, 0.0))
-            cols = jnp.concatenate([high, mid, high, mid, high, low], axis=0)
-            rows = jnp.where((at >= 0) & (at < PANEL), jnp.where(at == sub, 1.0, 0.0), rows)
-            done = rows
-            piv = heads[0, 0:1, :]
-            for j in range(PANEL):
-                here = sub == j
-                root = lax.rsqrt(piv)
-                inv = root * root
-                done = jnp.where(here, rows * root, done)
-                mult = jnp.where(here, 0.0, heads[0])
-                if j < PANEL - 1:
-                    head_rows = heads[1:, j : j + 1, :] * inv
-                    piv = heads[1, j + 1 : j + 2, :] - heads[0, j + 1 : j + 2, :] * head_rows[0]
-                    heads = jnp.where(here[None], head_rows, heads[1:] - mult[None] * head_rows)
-                scaled = rows[j : j + 1, :] * inv
-                rows = jnp.where(here, scaled, rows - mult * scaled)
-            high, mid, low = split(rows)
-            rhs = jnp.concatenate([high, high, mid, mid, low, high], axis=0)
-            change = lax.dot_general(cols, rhs, TN, preferred_element_type=F32)
-            ref[...] = jnp.where(inside, 0.0, ref[...]) - change
-            ref[pl.ds(k0, PANEL), :] = done
+        rows = ref[pl.ds(k0, PANEL), :]
+        heads = jnp.stack(
+            [
+                jnp.broadcast_to(jnp.sum(jnp.where(at == j, rows, 0.0), axis=1, keepdims=True), (PANEL, S))
+                for j in range(PANEL)
+            ]
+        )
+        high, mid, low = split(jnp.where(at >= PANEL, rows, 0.0))
+        cols = jnp.concatenate([high, mid, high, mid, high, low], axis=0)
+        rows = jnp.where((at >= 0) & (at < PANEL), jnp.where(at == sub, 1.0, 0.0), rows)
+        done = rows
+        piv = heads[0, 0:1, :]
+        for j in range(PANEL):
+            here = sub == j
+            root = lax.rsqrt(piv)
+            inv = root * root
+            done = jnp.where(here, rows * root, done)
+            mult = jnp.where(here, 0.0, heads[0])
+            if j < PANEL - 1:
+                head_rows = heads[1:, j : j + 1, :] * inv
+                piv = heads[1, j + 1 : j + 2, :] - heads[0, j + 1 : j + 2, :] * head_rows[0]
+                heads = jnp.where(here[None], head_rows, heads[1:] - mult[None] * head_rows)
+            scaled = rows[j : j + 1, :] * inv
+            rows = jnp.where(here, scaled, rows - mult * scaled)
+        high, mid, low = split(rows)
+        rhs = jnp.concatenate([high, high, mid, mid, low, high], axis=0)
+        change = lax.dot_general(cols, rhs, TN, preferred_element_type=F32)
+        ref[...] = jnp.where(inside, 0.0, ref[...]) - change
+        ref[pl.ds(k0, PANEL), :] = done
         return carry
 
     lax.fori_loop(0, S // PANEL, panel, 0)
-    for ref in mats:
-        ref[...] = jnp.where(tall_lane <= tall_row, ref[...], 0.0)
 
 
 class Op:
@@ -97,12 +94,12 @@
     l_op, l_start, r_op, r_start,
     l_out, r_out, ray_out,
     l_a, r_a,
-    l_xs, l_xt, l_mate_s, l_mate_r, l_side_s, l_side_r, l_y, l_m, l_sp,
-    r_xs, r_xt, r_ps, r_pr, r_y, r_m, r_sp, r_keep,
-    g_loc, g_one, g_sum, g_two, g_tot,
+    l_xs, l_xt, l_mate_s, l_mate_r, l_side_s, l_side_r, l_hand, l_y, l_sp,
+    r_xs, r_xt, r_ps, r_pr, r_y, r_sp, r_keep,
+    g_loc, g_one, g_sum, g_two, g_m, g_fac,
     l_asem, r_asem,
     gs_sem, gr_sem, fs_sem, fr_sem, ps_sem, pr_sem, xs_sem, xr_sem,
-    lgs_sem, lgr_sem, lms_sem, lmr_sem, lss_sem, lsr_sem,
+    lgs_sem, lgr_sem, lhs_sem, lhr_sem, lms_sem, lmr_sem, lss_sem, lsr_sem,
     a1s_sem, a1r_sem, a2s_sem, a2r_sem, a3s_sem, a3r_sem,
 ):
     y = lax.axis_index("row")
@@ -115,8 +112,8 @@
     tile = r_nb // TILES
     piece = r_nb // CHUNKS
 
-    left = Op(i=0, n=l_n, nb=l_nb, y=l_y, m=l_m, sp=l_sp)
-    right = Op(i=1, n=r_n, nb=r_nb, y=r_y, m=r_m, sp=r_sp)
+    left = Op(i=0, n=l_n, nb=l_nb, y=l_y, sp=l_sp)
+    right = Op(i=1, n=r_n, nb=r_nb, y=r_y, sp=r_sp)
     ops = [left, right]
 
     l_load = pltpu.make_async_copy(l_op, l_a, l_asem)
@@ -185,19 +182,36 @@
     def left_copy(b, slot):
         return remote(l_xs, l_xt.at[slot], lgs_sem.at[b], lgr_sem.at[slot], b, 2 * y + x)
 
+    def left_across(b):
+        return remote(l_xs, l_hand, lgs_sem.at[b], lhr_sem, 1 - y, col)
+
+    def left_hand_on():
+        return remote(l_hand, l_xt.at[k], lhs_sem, lgr_sem.at[k], y, 2 * (1 - x) + x)
+
     def left_self(b):
         return (b == y) & (y == x) & (x == k)
 
     def left_start():
-        for b in range(2):
+        for b in (1 - y, y):
+            across = (b != y) & (x != y)
 
             @pl.when(left_self(b))
             def _():
                 l_xt[k] = l_xs[...]
 
-            @pl.when(jnp.logical_not(left_self(b)))
+            @pl.when(across)
+            def _():
+                left_across(b).start()
+
+            @pl.when(jnp.logical_not(left_self(b) | across))
             def _():
                 left_copy(b, k).start()
+
+    def left_relay():
+        @pl.when(x == y)
+        def _():
+            left_across(0).wait_recv()
+            left_hand_on().start()
 
     def left_finish():
         for slot in range(2):
@@ -212,6 +226,10 @@
             @pl.when(jnp.logical_not(left_self(b)))
             def _():
                 left_copy(b, k).wait_send()
+
+        @pl.when(x == y)
+        def _():
+            left_hand_on().wait_send()
 
     def left_block(index):
         rows = pl.ds(pl.multiple_of(index * l_nb, l_nb), l_nb)
@@ -280,34 +298,54 @@
         for t in range(TILES):
             right_send(t).wait_send()
 
-    def all_reduce(par):
-        half, other = pl.ds(pl.multiple_of(k * 64, 64), 64), pl.ds(pl.multiple_of((1 - k) * 64, 64), 64)
-        one = remote(g_loc.at[:, other], g_one.at[par], a1s_sem.at[par], a1r_sem.at[par], y, mate)
+    low_lane = lax.broadcasted_iota(jnp.int32, (32, S), 1)
+    tall_row = lax.broadcasted_iota(jnp.int32, (S, S), 0)
+    tall_lane = lax.broadcasted_iota(jnp.int32, (S, S), 1)
+    count = jnp.where(k == 0, float(l_n), float(r_n))
+
+    def pack(i, gram):
+        g_loc[i, :64, :] = gram[:64]
+        g_loc[i, 64:96, :] = jnp.where(low_lane < 64, pltpu.roll(gram[64:96], 64, axis=1), gram[96:])
+
+    def sum_across(par, rows, after_sends):
+        part = pl.ds(0, rows)
+        one = remote(g_loc.at[1 - k, part], g_one.at[par, part], a1s_sem.at[par], a1r_sem.at[par], y, mate)
         one.start()
         one.wait_recv()
-        g_sum[...] = g_loc[:, half, :] + g_one[par]
+        g_sum[part, :] = g_loc[k, part, :] + g_one[par, part, :]
         twos = []
         for q in (2, 1, 0):
             yd = y + ((q + 1) // 2) * (1 - 2 * y)
             xd = x + ((q + 1) % 2) * (1 - 2 * x)
-            two = remote(g_sum, g_two.at[par, q], a2s_sem.at[par, q], a2r_sem.at[par, q], yd, 2 * xd + k)
+            two = remote(
+                g_sum.at[part], g_two.at[par, q, part], a2s_sem.at[par, q], a2r_sem.at[par, q], yd, 2 * xd + k
+            )
             two.start()
             twos.append(two)
+        after_sends()
         for two in twos:
             two.wait_recv()
-        g_tot[:, half, :] = (g_sum[...] + g_two[par, 0]) + (g_two[par, 1] + g_two[par, 2])
-        three = remote(g_tot.at[:, half], g_tot.at[:, half], a3s_sem.at[par], a3r_sem.at[par], y, mate)
-        three.start()
-        remote(g_tot.at[:, other], g_tot.at[:, other], a3s_sem.at[par], a3r_sem.at[par], y, mate).wait_recv()
+        total = (g_sum[part, :] + g_two[par, 0, part, :]) + (g_two[par, 1, part, :] + g_two[par, 2, part, :])
         one.wait_send()
         for two in twos:
             two.wait_send()
-        three.wait_send()
-
-    def factor():
-        for o in ops:
-            o.m[...] = g_tot[o.i] / float(o.n)
-        inverse_factors([o.m for o in ops])
+        return total / count
+
+    def hand_over(par):
+        mine, other = g_fac.at[k], g_fac.at[1 - k]
+        copy = remote(mine, mine, a3s_sem.at[par], a3r_sem.at[par], y, mate)
+        copy.start()
+        remote(other, other, a3s_sem.at[par], a3r_sem.at[par], y, mate).wait_recv()
+        copy.wait_send()
+
+    def factor(par):
+        gram = sum_across(par, 96, lambda: None)
+        g_m[:64, :] = gram[:64]
+        g_m[64:96, :] = pltpu.roll(gram[64:], 64, axis=1)
+        g_m[96:, :] = gram[64:]
+        inverse_factor(g_m)
+        g_fac[k] = jnp.where(tall_lane <= tall_row, g_m[...], 0.0)
+        hand_over(par)
 
     def apply_piece(o, lhs, start, width):
         high, mid, low = split(o.y[:, start : start + width])
@@ -315,7 +353,7 @@
         return dot(lhs, rhs)
 
     def apply_lhs(o):
-        high, mid, low = split(o.m[...])
+        high, mid, low = split(g_fac[o.i])
         return jnp.concatenate([high, mid, high, mid, high, low], axis=1)
 
     def second_gram(o):
@@ -328,7 +366,7 @@
                 o.sp[q * S : (q + 1) * S, start : start + 256] = parts[q]
         both = dot_nt(o.sp[: 2 * S, :], o.sp[: 2 * S, :])
         cross = dot_nt(o.sp[:S, :], o.sp[2 * S :, :])
-        g_loc[o.i] = both[:S, :S] + ((both[:S, S:] + both[S:, :S]) + (both[S:, S:] + (cross + cross.T)))
+        pack(o.i, both[:S, :S] + ((both[:S, S:] + both[S:, :S]) + (both[S:, S:] + (cross + cross.T))))
 
     def rayleigh(o, basis):
         g_loc[o.i] = lax.dot_general(basis, o.y[...], NT, precision=lax.Precision.HIGHEST, preferred_element_type=F32)
@@ -348,16 +386,15 @@
             l_xs[:, start : start + 256] = res.astype(BF16)
         left_start()
 
-    def multiply(gather, last):
-        gather.finish()
+    def multiply(last):
         right_multiply(0, last)
+        left_relay()
+        right_multiply(1, last)
         left_finish()
         left_multiply()
-        right_multiply(1, last)
         left_reduce_start()
         right_reduce_finish()
         left_reduce_finish()
-        gather.drain()
         left_drain()
 
     first, later = Gather(True), Gather(False)
@@ -372,24 +409,15 @@
     first.drain()
     l_load.wait()
 
-    class Ready:
-        def finish(self):
-            pass
-
-        def drain(self):
-            pass
-
     def sweep(i, carry):
-        multiply(Ready(), False)
+        multiply(False)
         for o in ops:
             half = o.y[...].astype(BF16)
-            g_loc[o.i] = dot_nt(half, half)
-        all_reduce(0)
-        factor()
+            pack(o.i, dot_nt(half, half))
+        factor(0)
         for o in ops:
             second_gram(o)
-        all_reduce(1)
-        factor()
+        factor(1)
         new_basis(later)
         later.finish()
         later.drain()
@@ -401,21 +429,22 @@
     home = remote(r_keep.at[0], r_keep.at[1], xs_sem, xr_sem, x, 2 * k + y)
     r_keep[0] = r_y[...]
 
-    @pl.when(stays)
-    def _():
-        r_keep[1] = r_y[...]
-
-    @pl.when(jnp.logical_not(stays))
-    def _():
-        home.start()
+    def start_home():
+        @pl.when(stays)
+        def _():
+            r_keep[1] = r_keep[0]
+
+        @pl.when(jnp.logical_not(stays))
+        def _():
+            home.start()
 
     l_out[...] = l_y[...]
-    multiply(Ready(), True)
+    multiply(True)
     rayleigh(left, l_out[...])
     rayleigh(right, r_keep[0])
-    all_reduce(0)
-    for o in ops:
-        ray_out[o.i] = g_tot[o.i] / float(o.n)
+    g_fac[k] = sum_across(2, S, start_home)
+    hand_over(2)
+    ray_out[...] = g_fac[...]
 
     @pl.when(jnp.logical_not(stays))
     def _():
@@ -454,27 +483,27 @@
                 pltpu.VMEM((2, S, l_nb), F32),
                 pltpu.VMEM((S, l_nb), F32),
                 pltpu.VMEM((S, l_nb), F32),
+                pltpu.VMEM((S, l_nb), BF16),
                 pltpu.VMEM((S, l_nb), F32),
-                pltpu.VMEM((S, S), F32),
                 pltpu.VMEM((3 * S, l_nb), BF16),
                 pltpu.VMEM((CHUNKS, S, r_nb // CHUNKS), BF16),
                 pltpu.VMEM((4, CHUNKS, S, r_nb // CHUNKS), BF16),
                 pltpu.VMEM((TILES, S, r_nb // TILES), F32),
                 pltpu.VMEM((TILES, S, r_nb // TILES), F32),
                 pltpu.VMEM((S, r_nb), F32),
-                pltpu.VMEM((S, S), F32),
                 pltpu.VMEM((3 * S, r_nb), BF16),
                 pltpu.VMEM((2, S, r_nb), F32),
                 pltpu.VMEM((2, S, S), F32),
-                pltpu.VMEM((2, 2, 64, S), F32),
-                pltpu.VMEM((2, 64, S), F32),
-                pltpu.VMEM((2, 3, 2, 64, S), F32),
+                pltpu.VMEM((3, S, S), F32),
+                pltpu.VMEM((S, S), F32),
+                pltpu.VMEM((3, 3, S, S), F32),
+                pltpu.VMEM((S, S), F32),
                 pltpu.VMEM((2, S, S), F32),
                 dma, dma((RING,)),
                 dma((2, CHUNKS)), dma((2, CHUNKS)), dma((2, CHUNKS)), dma((2, CHUNKS)),
                 dma((TILES,)), dma((TILES,)), dma, dma,
-                dma((2,)), dma((2,)), dma((2,)), dma((2,)), dma, dma,
-                dma((2,)), dma((2,)), dma((2, 3)), dma((2, 3)), dma((2,)), dma((2,)),
+                dma((2,)), dma((2,)), dma, dma, dma((2,)), dma((2,)), dma, dma,
+                dma((3,)), dma((3,)), dma((3, 3)), dma((3, 3)), dma((3,)), dma((3,)),
             ],
             compiler_params=pltpu.CompilerParams(has_side_effects=True, vmem_limit_bytes=64 * 1024 * 1024 - 65536),
         )(left_op, left_start, right_op, right_start)

time: 355 us -> 334 us (0.941)
  the two profiles are of different devices: /device:TPU:0 before, /device:TPU:1 now
where the time goes in v4:
time: 334 us; the launch traced here: 333 us
  Pallas kernels  333 us (100%)
    pallas_call x1, Pallas kernels, local_program(): pl.pallas_call(kernel, out_shape=(shape((S, l_nb), F32), shape((S, r_nb),...  330 us

profile of v4, /device:TPU:1, one launch (start us, length us, event | category | flops | bytes accessed | tf_op | source)
XLA Modules:
  0.0 333.4 jit_solution(10747048146594655712)
XLA Ops:
  0.6 330.0 %shard_map.75 = (f32[128,768]{1,0:T(8,128)}, f32[128,2048]{1,0:T(8,128)}, f32[2,128,128]{2,1,0:T(8,128)}) custom-call(bf16[3072,1536]{1,0:T(8,128)(2,1)} %l_op.1, f32[768,128]{1,0:T(8,128)} %l_start.1, bf16[8192,4096]{1,0:T(8,128)(2,1)} %r_op.1, f32[2048,128]{1,0:T(8,128)} %r_start.1), custom_call_target="tpu_custom_call" | custom-call | tf_op jit(solution)/shard_map/pallas_call | solution.py:472
  330.6 2.8 shard_map.76

commit v5 on v4

--- a/solution.py
+++ b/solution.py
@@ -1,3 +1,5 @@
+import functools
+
 import jax
 import jax.numpy as jnp
 from jax import lax
@@ -98,7 +100,7 @@
     r_xs, r_xt, r_ps, r_pr, r_y, r_sp, r_keep,
     g_loc, g_one, g_sum, g_two, g_m, g_fac,
     l_asem, r_asem,
-    gs_sem, gr_sem, fs_sem, fr_sem, ps_sem, pr_sem, xs_sem, xr_sem,
+    gs_sem, gr_sem, fs_sem, fr_sem, ps_sem, pr_sem, xs_sem, xr_sem, es_sem, er_sem,
     lgs_sem, lgr_sem, lhs_sem, lhr_sem, lms_sem, lmr_sem, lss_sem, lsr_sem,
     a1s_sem, a1r_sem, a2s_sem, a2r_sem, a3s_sem, a3r_sem,
 ):
@@ -242,20 +244,19 @@
         return remote(l_side_s, l_side_r, lss_sem, lsr_sem, y, 2 * (1 - x) + k)
 
     def left_multiply():
-        for a in (1 - x, x):
-            l_mate_s[a] = left_block(2 * a + (1 - k))
-            left_mate(a).start()
+        l_mate_s[1 - x] = left_block(2 * (1 - x) + (1 - k))
+        left_mate(1 - x).start()
         l_side_s[...] = left_block(2 * (1 - x) + k)
-        l_y[...] = left_block(2 * x + k)
-
-    def left_reduce_start():
+        l_mate_s[x] = left_block(2 * x + (1 - k))
+        left_mate(x).start()
         left_mate(1 - x).wait_recv()
         l_side_s[...] = l_side_s[...] + l_mate_r[1 - x]
         left_side().start()
+        l_y[...] = left_block(2 * x + k)
+
+    def left_reduce_finish():
         left_mate(x).wait_recv()
         l_y[...] = l_y[...] + l_mate_r[x]
-
-    def left_reduce_finish():
         left_side().wait_recv()
         l_y[...] = l_y[...] + l_side_r[...]
         left_side().wait_send()
@@ -275,7 +276,7 @@
                 total = part if total is None else total + part
         return total
 
-    def right_multiply(own, last):
+    def right_multiply(own, last, begin=0, end=TILES):
         def one(i, carry):
             t = i + TILES * own
             res = right_tile(t)
@@ -283,13 +284,14 @@
                 r_y[:, pl.ds(pl.multiple_of(i * tile, tile), tile)] = res
             else:
                 r_ps[i] = res
-                right_send(i).start()
+                if not last:
+                    right_send(i).start()
             ahead = t + RING
             if not (last and own):
                 r_fetch(lax.rem(ahead, 2 * TILES)).start()
             return carry
 
-        lax.fori_loop(0, TILES, one, 0)
+        lax.fori_loop(begin, end, one, 0)
 
     def right_reduce_finish():
         for t in range(TILES):
@@ -307,11 +309,12 @@
         g_loc[i, :64, :] = gram[:64]
         g_loc[i, 64:96, :] = jnp.where(low_lane < 64, pltpu.roll(gram[64:96], 64, axis=1), gram[96:])
 
-    def sum_across(par, rows, after_sends):
+    def sum_across(par, rows):
         part = pl.ds(0, rows)
         one = remote(g_loc.at[1 - k, part], g_one.at[par, part], a1s_sem.at[par], a1r_sem.at[par], y, mate)
         one.start()
-        one.wait_recv()
+        with jax.named_scope("ar_one"):
+            one.wait_recv()
         g_sum[part, :] = g_loc[k, part, :] + g_one[par, part, :]
         twos = []
         for q in (2, 1, 0):
@@ -322,30 +325,43 @@
             )
             two.start()
             twos.append(two)
-        after_sends()
-        for two in twos:
-            two.wait_recv()
+        with jax.named_scope("ar_two"):
+            for two in twos:
+                two.wait_recv()
         total = (g_sum[part, :] + g_two[par, 0, part, :]) + (g_two[par, 1, part, :] + g_two[par, 2, part, :])
         one.wait_send()
         for two in twos:
             two.wait_send()
         return total / count
 
-    def hand_over(par):
+    def hand_over(par, left_work, right_work):
         mine, other = g_fac.at[k], g_fac.at[1 - k]
         copy = remote(mine, mine, a3s_sem.at[par], a3r_sem.at[par], y, mate)
+        back = remote(other, other, a3s_sem.at[par], a3r_sem.at[par], y, mate)
         copy.start()
-        remote(other, other, a3s_sem.at[par], a3r_sem.at[par], y, mate).wait_recv()
+
+        @pl.when(k == 0)
+        def _():
+            left_work()
+            back.wait_recv()
+            right_work()
+
+        @pl.when(k == 1)
+        def _():
+            right_work()
+            back.wait_recv()
+            left_work()
+
         copy.wait_send()
 
     def factor(par):
-        gram = sum_across(par, 96, lambda: None)
+        gram = sum_across(par, 96)
         g_m[:64, :] = gram[:64]
         g_m[64:96, :] = pltpu.roll(gram[64:], 64, axis=1)
         g_m[96:, :] = gram[64:]
-        inverse_factor(g_m)
+        with jax.named_scope("chol"):
+            inverse_factor(g_m)
         g_fac[k] = jnp.where(tall_lane <= tall_row, g_m[...], 0.0)
-        hand_over(par)
 
     def apply_piece(o, lhs, start, width):
         high, mid, low = split(o.y[:, start : start + width])
@@ -368,34 +384,45 @@
         cross = dot_nt(o.sp[:S, :], o.sp[2 * S :, :])
         pack(o.i, both[:S, :S] + ((both[:S, S:] + both[S:, :S]) + (both[S:, S:] + (cross + cross.T))))
 
-    def rayleigh(o, basis):
-        g_loc[o.i] = lax.dot_general(basis, o.y[...], NT, precision=lax.Precision.HIGHEST, preferred_element_type=F32)
-
-    def new_basis(gather):
+    def high_dot_nt(lhs, rhs):
+        return lax.dot_general(lhs, rhs, NT, precision=lax.Precision.HIGHEST, preferred_element_type=F32)
+
+    def new_left():
+        lhs = apply_lhs(left)
+        for start in range(0, l_nb, 256):
+            res = apply_piece(left, lhs, start, 256)
+            l_y[:, start : start + 256] = res
+            l_xs[:, start : start + 256] = res.astype(BF16)
+
+    def new_right():
         lhs = apply_lhs(right)
         for h in range(CHUNKS):
             for start in range(h * piece, (h + 1) * piece, 256):
                 res = apply_piece(right, lhs, start, 256)
                 r_y[:, start : start + 256] = res
                 r_xs[h, :, start - h * piece : start - h * piece + 256] = res.astype(BF16)
-            gather.start(h)
-        lhs = apply_lhs(left)
-        for start in range(0, l_nb, 256):
-            res = apply_piece(left, lhs, start, 256)
-            l_y[:, start : start + 256] = res
-            l_xs[:, start : start + 256] = res.astype(BF16)
-        left_start()
-
-    def multiply(last):
-        right_multiply(0, last)
-        left_relay()
-        right_multiply(1, last)
-        left_finish()
-        left_multiply()
-        left_reduce_start()
-        right_reduce_finish()
-        left_reduce_finish()
+            later.start(h)
+
+    def multiply(drain, last):
+        with jax.named_scope("r_mul0"):
+            right_multiply(0, last)
+        with jax.named_scope("l_relay"):
+            left_relay()
+        with jax.named_scope("r_mul1"):
+            right_multiply(1, last, 0, 2)
+        with jax.named_scope("l_fin"):
+            left_finish()
+        with jax.named_scope("l_mul"):
+            left_multiply()
+        with jax.named_scope("r_mul2"):
+            right_multiply(1, last, 2, TILES)
+        if not last:
+            with jax.named_scope("r_red"):
+                right_reduce_finish()
+        with jax.named_scope("l_red"):
+            left_reduce_finish()
         left_drain()
+        drain()
 
     first, later = Gather(True), Gather(False)
     for h in range(CHUNKS):
@@ -405,53 +432,92 @@
     for b in range(l_nb // S):
         l_xs[:, b * S : (b + 1) * S] = l_start[b * S : (b + 1) * S, :].T.astype(BF16)
     left_start()
-    first.finish()
+    with jax.named_scope("gather_first"):
+        first.finish()
     first.drain()
     l_load.wait()
 
     def sweep(i, carry):
-        multiply(False)
-        for o in ops:
-            half = o.y[...].astype(BF16)
-            pack(o.i, dot_nt(half, half))
-        factor(0)
-        for o in ops:
-            second_gram(o)
-        factor(1)
-        new_basis(later)
-        later.finish()
-        later.drain()
+        multiply(functools.partial(pl.when(i > 0), later.drain), False)
+        with jax.named_scope("gram1"):
+            for o in ops:
+                half = o.y[...].astype(BF16)
+                pack(o.i, dot_nt(half, half))
+        with jax.named_scope("factor0"):
+            factor(0)
+        with jax.named_scope("gram2"):
+            hand_over(0, lambda: second_gram(left), lambda: second_gram(right))
+        with jax.named_scope("factor1"):
+            factor(1)
+        with jax.named_scope("new_basis"):
+            hand_over(1, new_left, new_right)
+            left_start()
+        with jax.named_scope("gather"):
+            later.finish()
         return carry
 
     lax.fori_loop(0, SWEEPS, sweep, 0)
 
-    stays = (x == y) & (col == 2 * k + y)
-    home = remote(r_keep.at[0], r_keep.at[1], xs_sem, xr_sem, x, 2 * k + y)
-    r_keep[0] = r_y[...]
-
-    def start_home():
-        @pl.when(stays)
+    stays = (x == y) & (k == y)
+
+    def swap(c):
+        return remote(r_keep.at[0, c], r_keep.at[1, c], es_sem.at[c], er_sem.at[c], 1 - y, col)
+
+    def home(q, c):
+        place = 2 * k + (y if q == 0 else 1 - y)
+        return remote(r_keep.at[q, c], r_pr.at[c], xs_sem.at[q, c], xr_sem.at[c], y, place)
+
+    for c in range(TILES):
+        r_keep[0, c] = r_y[:, c * tile : (c + 1) * tile]
+        swap(c).start()
+
+        @pl.when((x == y) & (k != y))
         def _():
-            r_keep[1] = r_keep[0]
-
-        @pl.when(jnp.logical_not(stays))
-        def _():
-            home.start()
+            home(0, c).start()
 
     l_out[...] = l_y[...]
-    multiply(True)
-    rayleigh(left, l_out[...])
-    rayleigh(right, r_keep[0])
-    g_fac[k] = sum_across(2, S, start_home)
-    hand_over(2)
+    with jax.named_scope("last_mul"):
+        multiply(later.drain, True)
+    with jax.named_scope("ray"):
+        g_loc[0] = high_dot_nt(l_out[...], l_y[...])
+        total = None
+        for c in range(TILES):
+            part = high_dot_nt(r_keep[0, c], r_y[:, c * tile : (c + 1) * tile])
+            total = part if total is None else total + part
+        for c in range(TILES):
+            swap(c).wait_recv()
+
+            @pl.when(x == y)
+            def _():
+                home(1, c).start()
+
+            total = total + high_dot_nt(r_keep[1, c], r_ps[c])
+        g_loc[1] = total
+    with jax.named_scope("last_sum"):
+        g_fac[k] = sum_across(2, S)
+    with jax.named_scope("last_hand"):
+        hand_over(2, lambda: None, lambda: None)
     ray_out[...] = g_fac[...]
-
-    @pl.when(jnp.logical_not(stays))
-    def _():
-        home.wait_recv()
-        home.wait_send()
-
-    r_out[...] = r_keep[1]
+    with jax.named_scope("home"):
+        for c in range(TILES):
+            swap(c).wait_send()
+
+            @pl.when(x == y)
+            def _():
+                home(1, c).wait_send()
+
+            @pl.when((x == y) & (k != y))
+            def _():
+                home(0, c).wait_send()
+
+            @pl.when(stays)
+            def _():
+                r_out[:, c * tile : (c + 1) * tile] = r_keep[0, c]
+
+            @pl.when(jnp.logical_not(stays))
+            def _():
+                home(0, c).wait_recv()
+                r_out[:, c * tile : (c + 1) * tile] = r_pr[c]
 
 
 def finish_kernel(l_in, r_in, ray_in, l_out, l_ray, r_out, r_ray):
@@ -492,7 +558,7 @@
                 pltpu.VMEM((TILES, S, r_nb // TILES), F32),
                 pltpu.VMEM((S, r_nb), F32),
                 pltpu.VMEM((3 * S, r_nb), BF16),
-                pltpu.VMEM((2, S, r_nb), F32),
+                pltpu.VMEM((2, TILES, S, r_nb // TILES), F32),
                 pltpu.VMEM((2, S, S), F32),
                 pltpu.VMEM((3, S, S), F32),
                 pltpu.VMEM((S, S), F32),
@@ -501,7 +567,7 @@
                 pltpu.VMEM((2, S, S), F32),
                 dma, dma((RING,)),
                 dma((2, CHUNKS)), dma((2, CHUNKS)), dma((2, CHUNKS)), dma((2, CHUNKS)),
-                dma((TILES,)), dma((TILES,)), dma, dma,
+                dma((TILES,)), dma((TILES,)), dma((2, TILES)), dma((TILES,)), dma((TILES,)), dma((TILES,)),
                 dma((2,)), dma((2,)), dma, dma, dma((2,)), dma((2,)), dma, dma,
                 dma((3,)), dma((3,)), dma((3, 3)), dma((3, 3)), dma((3,)), dma((3,)),
             ],

time: 334 us -> 323 us (0.967)
  the two profiles are of different devices: /device:TPU:1 before, /device:TPU:0 now
where the time goes in v5:
time: 323 us
  Pallas kernels  322 us (100%)
    pallas_call x1, Pallas kernels, local_program(): pl.pallas_call(kernel, out_shape=(shape((S, l_nb), F32), shape((S, r_nb),...  319 us

profile of v5, /device:TPU:0, one launch (start us, length us, event | category | flops | bytes accessed | tf_op | source)
XLA Modules:
  0.0 322.6 jit_solution(2062079400907654180)
XLA Ops:
  0.6 319.2 %shard_map.75 = (f32[128,768]{1,0:T(8,128)}, f32[128,2048]{1,0:T(8,128)}, f32[2,128,128]{2,1,0:T(8,128)}) custom-call(bf16[3072,1536]{1,0:T(8,128)(2,1)} %l_op.1, f32[768,128]{1,0:T(8,128)} %l_start.1, bf16[8192,4096]{1,0:T(8,128)(2,1)} %r_op.1, f32[2048,128]{1,0:T(8,128)} %r_start.1), custom_call_target="tpu_custom_call" | custom-call | tf_op jit(solution)/shard_map/pallas_call | solution.py:538
  319.8 2.8 shard_map.76
